TPU v7x, 32 devices: a whole 2x2x4 slice. The times are simulated.
32 devices in a mesh: row: 16 (over z, x, core), col: 2 (over y).
Axes of the slice: x: 2, y: 2, z: 4, core: 2. Of those that a mesh axis runs over, the one named last changes fastest.
Arguments:
- occupied_waves: bfloat16 [1024, 32768], P('row', 'col'), may hold values from -6 to 6
- virtual_waves: bfloat16 [512, 32768], P('row', 'col'), may hold values from -6 to 6
- occupied_decay: float32 [1024], replicated, may hold values from 0.02 to 1
- virtual_decay: float32 [512], replicated, may hold values from 0.02 to 1
Outputs:
- spectrum_real: float32 [512, 32, 1024], P('row', 'col')
- spectrum_imaginary: float32 [512, 32, 1024], P('row', 'col')
All inputs are finite; a program needn't handle non-finite values.
Results may differ from a plain program's by a relative error of at most 0.0041.
Values may be sent and summed in bfloat16 or wider, within the bound.
A program may use at most 128 MiB of HBM per device.

v0:
```python
import functools
import math

import jax
import jax.numpy as jnp
import numpy as np
from jax import lax
from jax.experimental import pallas as pl
from jax.experimental.pallas import tpu as pltpu
from jax.sharding import PartitionSpec as P

NA = 32
NB = 32
NC = 32
NAB = NA * NB
NGRID = NA * NB * NC
LANES = 128
R_BLOCK = 16


def trig(phase, length):
    angle = (phase % length) * (2.0 * math.pi / length)
    return np.cos(angle), np.sin(angle)


def bf16_table(table):
    return jnp.asarray(table.astype(np.float32)).astype(jnp.bfloat16)


def plane_tables():
    index = np.arange(NAB)
    a, b = index // NB, index % NB
    phase = a[:, None] * a[None, :] * NB + b[:, None] * b[None, :] * NA
    cosine, sine = trig(phase, NA * NB)
    return bf16_table(cosine), bf16_table(sine)


def line_tables(col_count):
    share = NC // col_count
    full = np.zeros((col_count, 2, R_BLOCK, share, NC, R_BLOCK))
    for y in range(col_count):
        kc = y * share + np.arange(share)
        cosine, sine = trig(kc[:, None] * np.arange(NC)[None, :], NC)
        for r in range(R_BLOCK):
            full[y, 0, r, :, :, r] = cosine
            full[y, 1, r, :, :, r] = -sine
    return bf16_table(full.reshape(col_count, 2 * R_BLOCK * share, NC * R_BLOCK))


def swap_table(outer, inner, width):
    index = np.arange(outer * inner * width).reshape(outer, inner, width)
    source = np.transpose(index, (1, 0, 2)).reshape(-1)
    table = np.zeros((source.size, source.size))
    table[source, np.arange(source.size)] = 1.0
    return bf16_table(table)


def dot(a, b):
    return jnp.dot(a, b, preferred_element_type=jnp.float32)


def spectrum_kernel(pieces, x_ref, swap_ref, line_ref, cos_ref, sin_ref, re_ref, im_ref, rows):
    if pieces:
        per = LANES // NB
        for g in range(NA // per):
            parts = []
            for t in range(NC // per):
                lanes = pl.ds(t * LANES, LANES)
                parts.append(
                    jnp.concatenate([x_ref[g * per + k, :, lanes] for k in range(per)], axis=1)
                )
            moved = dot(jnp.concatenate(parts, axis=0), swap_ref[...]).astype(jnp.bfloat16)
            for t in range(NC // per):
                for j in range(per):
                    rows[pl.ds((t * per + j) * R_BLOCK, R_BLOCK), pl.ds(g * LANES, LANES)] = moved[
                        t * R_BLOCK : (t + 1) * R_BLOCK, j * LANES : (j + 1) * LANES
                    ]
    else:
        rows[...] = x_ref[...].reshape(NC * R_BLOCK, NAB)
    line = dot(line_ref[lax.axis_index("col")], rows[...]).astype(jnp.bfloat16)
    half = line.shape[0] // 2
    re, im = line[:half], line[half:]
    re_ref[...] = dot(re, cos_ref[...]) + dot(im, sin_ref[...])
    im_ref[...] = dot(im, cos_ref[...]) - dot(re, sin_ref[...])


def spectrum(pieces, x, line_table):
    r_count = x.shape[1]
    cosine, sine = plane_tables()
    per = LANES // NB
    swap = swap_table(per, per, NB)
    out_rows = line_table.shape[1] // 2
    steps = r_count // R_BLOCK
    whole = lambda table: pl.BlockSpec(table.shape, lambda i: (0,) * table.ndim)
    out = jax.ShapeDtypeStruct((out_rows * steps, NAB), jnp.float32)
    out_spec = pl.BlockSpec((out_rows, NAB), lambda i: (i, 0))
    return pl.pallas_call(
        functools.partial(spectrum_kernel, pieces),
        grid=(steps,),
        in_specs=[
            pl.BlockSpec((x.shape[0], R_BLOCK, x.shape[2]), lambda i: (0, i, 0)),
            whole(swap),
            whole(line_table),
            whole(cosine),
            whole(sine),
        ],
        out_specs=[out_spec, out_spec],
        out_shape=[out, out],
        scratch_shapes=[pltpu.VMEM((NC * R_BLOCK, NAB), jnp.bfloat16)],
        compiler_params=pltpu.CompilerParams(vmem_limit_bytes=48 * 1024 * 1024),
    )(x, swap, line_table, cosine, sine)


MESH = pl.DeviceIdType.MESH


def flip(index, mask):
    bits = [1 << bit for bit in range(mask.bit_length()) if mask >> bit & 1]
    for bit in bits:
        index = index + bit - 2 * bit * lax.rem(lax.div(index, bit), 2)
    return index


def group_size(row_count):
    return 4 if row_count % 4 == 0 else 1


def enter(row_count, col_count, row, col):
    barrier = pltpu.get_barrier_semaphore()
    for k in range(1, row_count):
        target = (lax.rem(row + k, row_count), col)
        pl.semaphore_signal(barrier, inc=1, device_id=target, device_id_type=MESH)
    for k in range(1, col_count):
        target = (row, lax.rem(col + k, col_count))
        pl.semaphore_signal(barrier, inc=1, device_id=target, device_id_type=MESH)
    pl.semaphore_wait(barrier, row_count + col_count - 2)


def send(src, dst, send_sem, recv_sem, target):
    return pltpu.make_async_remote_copy(
        src_ref=src,
        dst_ref=dst,
        send_sem=send_sem,
        recv_sem=recv_sem,
        device_id=target,
        device_id_type=MESH,
    )


def gather_kernel(
    row_count,
    col_count,
    inner,
    occ_ref,
    vir_ref,
    occ_slab,
    vir_slab,
    occ_out,
    vir_out,
    occ_rows,
    vir_rows,
    wave_send,
    wave_recv,
    col_send,
    col_recv,
    line_send,
    line_recv,
    group_send,
    group_recv,
    local,
):
    row, col = lax.axis_index("row"), lax.axis_index("col")
    outer = row_count // inner
    mine, seat = lax.div(row, inner), lax.rem(row, inner)
    points = occ_ref.shape[1] // row_count
    waves = ((occ_ref, occ_out), (vir_ref, vir_out))
    slabs = ((occ_slab, occ_rows), (vir_slab, vir_rows))
    enter(row_count, col_count, row, col)

    def block(index):
        return pl.ds(pl.multiple_of(index * points, LANES), points)

    own = [
        pltpu.make_async_copy(src.at[:, block(row)], dst.at[row], local.at[i])
        for i, (src, dst) in enumerate(waves)
    ]
    for copy in own:
        copy.start()

    def over_col(i, k):
        src, dst = slabs[i]
        place = dst.at[mine, seat]
        return send(src, place, col_send.at[i, k], col_recv.at[i, 0], (row, k))

    @pl.when(col == 0)
    def _():
        for i, (src, dst) in enumerate(slabs):
            for k in range(1, col_count):
                over_col(i, k).start()
            pltpu.make_async_copy(src, dst.at[mine, seat], local.at[2 + i]).start()

    pending = []

    def start_waves(far, steps=range(inner)):
        for step in steps:
            if far == 0 and step == 0:
                continue
            k = far * inner + step
            there = flip(mine, far)
            to = there * inner + lax.rem(seat + step, inner)
            for i, (src, dst) in enumerate(waves):
                copy = send(
                    src.at[:, block(to)],
                    dst.at[row],
                    wave_send.at[i, k],
                    wave_recv.at[i, k],
                    (to, col),
                )
                copy.start()
                pending.append(copy)

    start_waves(0)

    @pl.when(col == 0)
    def _():
        for i, (src, dst) in enumerate(slabs):
            pltpu.make_async_copy(src, dst.at[mine, seat], local.at[2 + i]).wait()

    @pl.when(col != 0)
    def _():
        for i in range(2):
            over_col(i, 1).wait_recv()

    lines = []
    bits = [1 << bit for bit in reversed(range((outer - 1).bit_length()))]
    early = inner // 2

    def double(held, bit):
        to = (flip(mine, bit) * inner + seat, col)
        started = []
        for mask in held:
            for i in range(2):
                place = slabs[i][1].at[flip(mine, mask), seat]
                k = bit + mask
                started.append(send(place, place, line_send.at[i, k], line_recv.at[i, k], to))
        for copy in started:
            copy.start()
        lines.extend(started)
        return started

    held = [0]
    for number, bit in enumerate(bits):
        started = double(held, bit)
        if number == 0:
            start_waves(bits[0], range(early))
        held = held + [mask + bit for mask in held]
        if number == len(bits) - 1:
            for far in range(1, bits[0]):
                start_waves(far)
            start_waves(bits[0], range(early, inner))
        for copy in started:
            copy.wait_recv()
    groups = []
    for k in range(1, inner):
        to = (mine * inner + lax.rem(seat + k, inner), col)
        for i in range(2):
            place = slabs[i][1].at[:, seat]
            copy = send(place, place, group_send.at[i, k], group_recv.at[i, k], to)
            copy.start()
            groups.append(copy)
    for far in range(bits[0] + 1 if bits else 1, outer):
        start_waves(far)
    for copy in own:
        copy.wait()
    for copy in groups:
        copy.wait()
    for copy in lines:
        copy.wait_send()

    @pl.when(col == 0)
    def _():
        for i in range(2):
            for k in range(1, col_count):
                over_col(i, k).wait_send()

    for copy in pending:
        copy.wait()


def gather(row_count, col_count, occ, vir, occ_slab, vir_slab):
    inner = group_size(row_count)
    points = occ.shape[1] // row_count
    window = occ_slab.shape[1]
    outer = row_count // inner
    shapes = [(row_count, w.shape[0], points) for w in (occ, vir)]
    shapes += [(outer, inner, w.shape[0], window) for w in (occ, vir)]
    dma = pltpu.SemaphoreType.DMA
    return pl.pallas_call(
        functools.partial(gather_kernel, row_count, col_count, inner),
        out_shape=[jax.ShapeDtypeStruct(shape, jnp.bfloat16) for shape in shapes],
        in_specs=[pl.BlockSpec(memory_space=pltpu.HBM)] * 2
        + [pl.BlockSpec(memory_space=pltpu.VMEM)] * 2,
        out_specs=[pl.BlockSpec(memory_space=pltpu.VMEM)] * 4,
        scratch_shapes=[dma((2, row_count))] * 2
        + [dma((2, col_count))] * 2
        + [dma((2, outer))] * 2
        + [dma((2, inner))] * 2
        + [dma((4,))],
        compiler_params=pltpu.CompilerParams(
            collective_id=0, has_side_effects=True, vmem_limit_bytes=32 * 1024 * 1024
        ),
    )(occ, vir, occ_slab, vir_slab)


def deliver_kernel(
    row_count, col_count, p_ref, x_ref, row_send, row_recv, col_send, col_recv, local
):
    row, col = lax.axis_index("row"), lax.axis_index("col")
    enter(row_count, col_count, row, col)
    inner = group_size(row_count)
    mine, seat = lax.div(row, inner), lax.rem(row, inner)
    here = x_ref.at[col, row]
    own = pltpu.make_async_copy(p_ref.at[row], here, local.at[0])
    own.start()
    rows = []
    order = range(1, row_count)
    for k in order:
        to = flip(mine, k // inner) * inner + lax.rem(seat + k % inner, inner)
        copy = send(p_ref.at[to], here, row_send.at[k], row_recv.at[k], (to, col))
        copy.start()
        rows.append(copy)
    forwards = []

    def forward(k, src, slot):
        for d in range(1, col_count):
            to = (row, lax.rem(col + d, col_count))
            copy = send(src, slot, col_send.at[d, k], col_recv.at[d, k], to)
            copy.start()
            forwards.append(copy)

    forward(0, p_ref.at[row], here)
    for k, copy in zip(order, rows):
        copy.wait_recv()
        source = flip(mine, k // inner) * inner + lax.rem(seat + inner - k % inner, inner)
        slot = x_ref.at[col, source]
        forward(k, slot, slot)
    own.wait()
    for copy in rows:
        copy.wait_send()
    for copy in forwards:
        copy.wait()


def deliver(row_count, col_count, polar):
    dma = pltpu.SemaphoreType.DMA
    return pl.pallas_call(
        functools.partial(deliver_kernel, row_count, col_count),
        out_shape=jax.ShapeDtypeStruct((col_count,) + polar.shape, jnp.bfloat16),
        in_specs=[pl.BlockSpec(memory_space=pltpu.VMEM)],
        out_specs=pl.BlockSpec(memory_space=pltpu.VMEM),
        scratch_shapes=[dma((row_count,))] * 2 + [dma((col_count, row_count))] * 2 + [dma((1,))],
        cost_estimate=pl.CostEstimate(
            flops=0, bytes_accessed=32 * polar.size * col_count, transcendentals=0
        ),
        compiler_params=pltpu.CompilerParams(
            collective_id=1, has_side_effects=True, vmem_limit_bytes=32 * 1024 * 1024
        ),
    )(polar)


def on_device(rows_dev, occupied_waves, virtual_waves, occupied_decay, virtual_decay):
    row_count = lax.axis_size("row")
    col_count = lax.axis_size("col")
    nocc, nvir = occupied_decay.shape[0], virtual_decay.shape[0]
    window = rows_dev * row_count
    points = occupied_waves.shape[1] // row_count
    contract = (((0,), (0,)), ((), ()))
    factor = -1.0 / math.sqrt(nocc * nvir) / math.sqrt(NGRID)

    def slab(waves, decay):
        share = waves.shape[0]
        own = lax.dynamic_slice_in_dim(decay, lax.axis_index("row") * share, share)
        return (waves[:, :window].astype(jnp.float32) * own[:, None]).astype(jnp.bfloat16)

    plane_occ, plane_vir, occ_rows, vir_rows = gather(
        row_count,
        col_count,
        occupied_waves,
        virtual_waves,
        slab(occupied_waves, occupied_decay),
        slab(virtual_waves, virtual_decay),
    )
    plane_occ, plane_vir = plane_occ.reshape(nocc, points), plane_vir.reshape(nvir, points)
    occ_rows, vir_rows = occ_rows.reshape(nocc, window), vir_rows.reshape(nvir, window)
    green_occ = lax.dot_general(occ_rows, plane_occ, contract, preferred_element_type=jnp.float32)
    green_vir = lax.dot_general(vir_rows, plane_vir, contract, preferred_element_type=jnp.float32)
    polar = (green_occ * green_vir * factor).astype(jnp.bfloat16)
    polar = dot(polar, swap_table(points // NC, NC, 1)).astype(jnp.bfloat16)
    polar = polar.reshape(row_count, rows_dev, points)
    polar = deliver(row_count, col_count, polar)
    pieces = points == NB * NC
    if pieces:
        x = polar.reshape(col_count * row_count, rows_dev, points)
    else:
        x = polar.reshape(col_count * row_count, rows_dev, NC, points // NC)
        x = jnp.transpose(x, (2, 1, 0, 3)).reshape(NC, rows_dev, NAB)
    real_part, imag_part = spectrum(pieces, x, line_tables(col_count))
    shape = (rows_dev, NC // col_count, NAB)
    return real_part.reshape(shape), imag_part.reshape(shape)


ROWS_DEV = 32


def solution(mesh):
    in_specs = (P("row", "col"), P("row", "col"), P(), P())
    out_specs = (P("row", "col", None), P("row", "col", None))
    return jax.shard_map(
        functools.partial(on_device, ROWS_DEV),
        mesh=mesh,
        in_specs=in_specs,
        out_specs=out_specs,
        check_vma=False,
    )
```

profile of v0, /device:TPU:0, one launch (start us, length us, event | category | flops | bytes accessed | tf_op | source)
XLA Modules:
  0.0 138.2 jit_solution(5737233243685717459)
XLA Ops:
  0.6 0.8 dynamic_slice.7
  1.4 0.8 dynamic_slice.6
  2.2 0.8 multiply_convert_fusion.2.vir_slab
  3.0 0.9 multiply_convert_fusion.1.occ_slab
  3.9 0.0 copy-start
  3.9 1.6 %copy-done = bf16[64,16384]{1,0:T(8,128)(2,1)S(1)} copy-done((bf16[64,16384]{1,0:T(8,128)(2,1)S(1)}, bf16[64,16384]{1,0:T(8,128)(2,1)}, u32[]{:S(2)}) %copy-start) | copy-done | bytes 2097176
  5.5 0.0 copy-start.2
  5.5 1.2 copy-done.2
  6.7 68.8 %shard_map.104 = (bf16[16,64,1024]{2,1,0:T(8,128)(2,1)S(1)}, bf16[16,32,1024]{2,1,0:T(8,128)(2,1)S(1)}, bf16[4,4,64,512]{3,2,1,0:T(8,128)(2,1)S(1)}, bf16[4,4,32,512]{3,2,1,0:T(8,128)(2,1)S(1)}) custom-call(bf16[64,16384]{1,0:T(8,128)(2,1)S(1)} %copy-done, bf16[32,16384]{1,0:T(8,128)(2,1)S(1)} %copy-done.2, ...), custom_call_target="tpu_custom_call" | custom-call | tf_op jit(solution)/shard_map/pallas_call | solution.py:298
  75.5 2.6 %fusion.1 = f32[512,1024]{1,0:T(8,128)} fusion(bf16[1024,512]{1,0:T(8,128)(2,1)S(1)} %bitcast.15, bf16[1024,1024]{1,0:T(8,128)(2,1)S(1)} %bitcast.14), kind=kOutput, calls=%fused_computation.5 | convolution fusion | flops 1073741824 | bytes 5242880 | tf_op jit(solution)/shard_map/dot_general | solution.py:395
  78.1 0.0 copy-start.4
  78.1 4.1 %convolution_convert_fusion = bf16[512,1024]{1,0:T(8,128)(2,1)S(1)} fusion(bf16[1024,1024]{1,0:T(8,128)(2,1)} %constant.33, f32[512,1024]{1,0:T(8,128)} %fusion.1, bf16[512,512]{1,0:T(8,128)(2,1)S(1)} %bitcast.18, bf16[512,1024]{1,0:T(8,128)(2,1)S(1)} %bitcast.17), kind=kOutput, calls=%fused_computation.1 | convolution fusion | flops 1612709888 | bytes 6815744 | tf_op jit(solution)/shard_map/dot_general | solution.py:59
  82.2 0.0 copy-start.1
  82.2 0.0 copy-start.3
  82.3 46.2 %shard_map.105 = bf16[2,16,32,1024]{3,2,1,0:T(8,128)(2,1)S(1)} custom-call(bf16[16,32,1024]{2,1,0:T(8,128)(2,1)S(1)} %bitcast.16), custom_call_target="tpu_custom_call" | custom-call | bytes 33554432 | tf_op jit(solution)/shard_map/pallas_call | solution.py:356
  128.5 0.0 copy-done.4
  128.5 0.0 copy-done.1
  128.5 0.0 copy-done.3
  128.5 9.7 %shard_map.106 = (f32[512,1024]{1,0:T(8,128)}, f32[512,1024]{1,0:T(8,128)}) custom-call(bf16[32,32,1024]{2,1,0:T(8,128)(2,1)S(1)} %bitcast.13, bf16[512,512]{1,0:T(8,128)(2,1)S(1)} %copy-done.4, bf16[2,512,512]{2,1,0:T(8,128)(2,1)S(1)} %copy-done.3, bf16[1024,1024]{1,0:T(8,128)(2,1)S(1)} %copy-done.1, bf16[1024,1024]{1,0:T(8,128)(2,1)} %constant.37.sin_ref), custom_call_target="tpu_custom_call" | custom-call | tf_op jit(solution)/shard_map/pallas_call | solution.py:97
Async XLA Ops:
  3.9 1.6 %copy-start = (bf16[64,16384]{1,0:T(8,128)(2,1)S(1)}, bf16[64,16384]{1,0:T(8,128)(2,1)}, u32[]{:S(2)}) copy-start(bf16[64,16384]{1,0:T(8,128)(2,1)} %occ_ref.1) | copy-start | bytes 6291460
  5.5 1.2 copy-start.2
  78.1 50.4 %copy-start.4 = (bf16[512,512]{1,0:T(8,128)(2,1)S(1)}, bf16[512,512]{1,0:T(8,128)(2,1)}, u32[]{:S(2)}) copy-start(bf16[512,512]{1,0:T(8,128)(2,1)} %constant.34.swap_ref) | copy-start | bytes 1572868
  82.2 46.3 %copy-start.1 = (bf16[1024,1024]{1,0:T(8,128)(2,1)S(1)}, bf16[1024,1024]{1,0:T(8,128)(2,1)}, u32[]{:S(2)}) copy-start(bf16[1024,1024]{1,0:T(8,128)(2,1)} %constant.36.cos_ref) | copy-start | bytes 6291460
  82.2 46.3 %copy-start.3 = (bf16[2,512,512]{2,1,0:T(8,128)(2,1)S(1)}, bf16[2,512,512]{2,1,0:T(8,128)(2,1)}, u32[]{:S(2)}) copy-start(bf16[2,512,512]{2,1,0:T(8,128)(2,1)} %constant.35.line_ref) | copy-start | bytes 3145732
where the time goes:
time: 139 us; the launch traced here: 138 us
  Pallas kernels  125 us (90%)
  matrix products  6.68 us (5%)
  local copies, waits for them, and re-layouts  4.35 us (3%)
  other arithmetic  1.75 us (1%)
    pallas_call x1, Pallas kernels, gather(): pl.pallas_call(functools.partial(gather_kernel, row_count, col_count, inn...  68.8 us
    pallas_call x1, Pallas kernels, deliver(): pl.pallas_call(functools.partial(deliver_kernel, row_count, col_count), o...  46.2 us
    pallas_call x1, Pallas kernels, spectrum(): pl.pallas_call(functools.partial(spectrum_kernel, pieces), grid=(steps,),...  9.68 us
    dot_general x1, matrix products, dot(): return jnp.dot(a, b, preferred_element_type=jnp.float32)  4.09 us
    unnamed x10, local copies, waits for them, and re-layouts  2.83 us

commit v1 on v0

v1 whole, which is shorter than its diff:
```python
import functools
import math

import jax
import jax.numpy as jnp
import numpy as np
from jax import lax
from jax.experimental import pallas as pl
from jax.experimental.pallas import tpu as pltpu
from jax.sharding import PartitionSpec as P

NA = 32
NB = 32
NC = 32
NAB = NA * NB
NGRID = NA * NB * NC
LANES = 128
R_BLOCK = 16


def trig(phase, length):
    angle = (phase % length) * (2.0 * math.pi / length)
    return np.cos(angle), np.sin(angle)


def bf16_table(table):
    return jnp.asarray(table.astype(np.float32)).astype(jnp.bfloat16)


def plane_tables():
    index = np.arange(NAB)
    a, b = index // NB, index % NB
    phase = a[:, None] * a[None, :] * NB + b[:, None] * b[None, :] * NA
    cosine, sine = trig(phase, NA * NB)
    return bf16_table(cosine), bf16_table(sine)


def line_tables(col_count):
    share = NC // col_count
    full = np.zeros((col_count, 2, R_BLOCK, share, NC, R_BLOCK))
    for y in range(col_count):
        kc = y * share + np.arange(share)
        cosine, sine = trig(kc[:, None] * np.arange(NC)[None, :], NC)
        for r in range(R_BLOCK):
            full[y, 0, r, :, :, r] = cosine
            full[y, 1, r, :, :, r] = -sine
    return bf16_table(full.reshape(col_count, 2 * R_BLOCK * share, NC * R_BLOCK))


def dot(a, b):
    return jnp.dot(a, b, preferred_element_type=jnp.float32)


def spectrum_kernel(x_ref, line_ref, cos_ref, sin_ref, re_ref, im_ref):
    rows = x_ref[...].reshape(NC * R_BLOCK, NAB)
    line = dot(line_ref[lax.axis_index("col")], rows).astype(jnp.bfloat16)
    half = line.shape[0] // 2
    re, im = line[:half], line[half:]
    re_ref[...] = dot(re, cos_ref[...]) + dot(im, sin_ref[...])
    im_ref[...] = dot(im, cos_ref[...]) - dot(re, sin_ref[...])


def spectrum(x, line_table):
    r_count = x.shape[1]
    cosine, sine = plane_tables()
    out_rows = line_table.shape[1] // 2
    steps = r_count // R_BLOCK
    whole = lambda table: pl.BlockSpec(table.shape, lambda i: (0,) * table.ndim)
    out = jax.ShapeDtypeStruct((out_rows * steps, NAB), jnp.float32)
    out_spec = pl.BlockSpec((out_rows, NAB), lambda i: (i, 0))
    return pl.pallas_call(
        spectrum_kernel,
        grid=(steps,),
        in_specs=[
            pl.BlockSpec((x.shape[0], R_BLOCK, x.shape[2]), lambda i: (0, i, 0)),
            whole(line_table),
            whole(cosine),
            whole(sine),
        ],
        out_specs=[out_spec, out_spec],
        out_shape=[out, out],
        compiler_params=pltpu.CompilerParams(vmem_limit_bytes=48 * 1024 * 1024),
    )(x, line_table, cosine, sine)


MESH = pl.DeviceIdType.MESH
HALVES = 2
HALF_ROWS = R_BLOCK


def flip(index, mask):
    bits = [1 << bit for bit in range(mask.bit_length()) if mask >> bit & 1]
    for bit in bits:
        index = index + bit - 2 * bit * lax.rem(lax.div(index, bit), 2)
    return index


def group_size(row_count):
    return 4 if row_count % 4 == 0 else 1


def send(src, dst, send_sem, recv_sem, target):
    return pltpu.make_async_remote_copy(
        src_ref=src,
        dst_ref=dst,
        send_sem=send_sem,
        recv_sem=recv_sem,
        device_id=target,
        device_id_type=MESH,
    )


def enter(row_count, col_count, inner, row, col):
    barrier = pltpu.get_barrier_semaphore()
    mine, seat = lax.div(row, inner), lax.rem(row, inner)
    targets = [(lax.rem(row + k, row_count), col) for k in range(1, row_count)]
    targets += [
        (mine * inner + lax.rem(seat + s, inner), lax.rem(col + d, col_count))
        for d in range(1, col_count)
        for s in range(inner)
    ]
    for target in targets:
        pl.semaphore_signal(barrier, inc=1, device_id=target, device_id_type=MESH)
    return barrier, len(targets)


def fill(ref, values, rows):
    width = ref.shape[1]

    def step(i, carry):
        start = pl.multiple_of(i * rows, rows)
        row = lax.broadcasted_iota(jnp.int32, (rows, width), 0) + start
        lane = lax.broadcasted_iota(jnp.int32, (rows, width), 1)
        ref[pl.ds(start, rows), :] = jnp.where(values(row, lane), 1.0, 0.0).astype(jnp.bfloat16)
        return carry

    lax.fori_loop(0, ref.shape[0] // rows, step, 0)


def whole_kernel(cfg, *refs):
    (row_count, col_count, inner, cuts, factor, fused) = cfg
    refs = list(refs)
    take = lambda n: [refs.pop(0) for _ in range(n)]
    occ_ref, vir_ref, occ_decay, vir_decay = take(4)
    if fused:
        line_hbm, cos_hbm, sin_hbm = take(3)
        acc_re, acc_im = take(2)
    else:
        (x_ref,) = take(1)
    planes = take(2)
    raws = take(2)
    lefts = take(2)
    mixed, polar, swap = take(3)
    if fused:
        x_ref, piece_swap, line_ref, cos_ref, sin_ref, lines_buf = take(6)
        table_sem = take(1)[0]
    (wave_send, wave_recv, col_send, col_recv, line_send, line_recv, group_send, group_recv) = take(8)
    (give_send, give_recv, pass_send, pass_recv, local) = take(5)

    row, col = lax.axis_index("row"), lax.axis_index("col")
    outer = row_count // inner
    mine, seat = lax.div(row, inner), lax.rem(row, inner)
    points = occ_ref.shape[1] // row_count
    waves = (occ_ref, vir_ref)
    window = raws[0].shape[3]
    share = window // col_count
    block_rows = row_count * HALF_ROWS

    def peer(k):
        return flip(mine, k // inner) * inner + lax.rem(seat + k % inner, inner)

    def source(k):
        return flip(mine, k // inner) * inner + lax.rem(seat + inner - k % inner, inner)

    barrier, arrivals = enter(row_count, col_count, inner, row, col)

    own = []
    for i in range(2):
        lanes = pl.ds(pl.multiple_of(row * points, LANES), points)
        own.append(pltpu.make_async_copy(waves[i].at[:, lanes], planes[i].at[row], local.at[i]))
    if fused:
        own.append(pltpu.make_async_copy(line_hbm.at[col], line_ref, table_sem.at[0]))
        own.append(pltpu.make_async_copy(cos_hbm, cos_ref, table_sem.at[1]))
        own.append(pltpu.make_async_copy(sin_hbm, sin_ref, table_sem.at[2]))
    for copy in own:
        copy.start()
    pl.semaphore_wait(barrier, arrivals)

    waiting = []

    def start_waves(part):
        first, last = cuts[part], cuts[part + 1]
        for k in range(row_count - 1, 0, -1):
            to = peer(k)
            lanes = pl.ds(pl.multiple_of(to * points + first, LANES), last - first)
            for i in range(2):
                copy = send(
                    waves[i].at[:, lanes],
                    planes[i].at[row, :, pl.ds(first, last - first)],
                    wave_send.at[i, part, k],
                    wave_recv.at[i, part, k],
                    (to, col),
                )
                copy.start()
                waiting.append((part, copy))

    def wait_waves(part):
        for number, copy in waiting:
            if number == part:
                copy.wait_recv()

    parts = len(cuts) - 1

    def slab_share(c):
        return pl.ds(c * share, share) if isinstance(c, int) else pl.ds(pl.multiple_of(c * share, LANES), share)

    def over_col(i, c):
        return send(
            waves[i].at[:, slab_share(c)],
            raws[i].at[mine, seat, :, slab_share(c)],
            col_send.at[i, c],
            col_recv.at[i, 0],
            (row, c),
        )

    @pl.when(col == 0)
    def _():
        for i in range(2):
            for c in range(1, col_count):
                over_col(i, c).start()
            pltpu.make_async_copy(
                waves[i].at[:, slab_share(0)], raws[i].at[mine, seat, :, slab_share(0)], local.at[2 + i]
            ).start()

    start_waves(0)

    @pl.when(col == 0)
    def _():
        for i in range(2):
            pltpu.make_async_copy(
                waves[i].at[:, slab_share(0)], raws[i].at[mine, seat, :, slab_share(0)], local.at[2 + i]
            ).wait()

    if col_count > 1:

        @pl.when(col != 0)
        def _():
            for i in range(2):
                over_col(i, 1).wait_recv()

    sent = []
    held = [0]
    bits = [1 << bit for bit in reversed(range((outer - 1).bit_length()))]
    next_part = 1
    for bit in bits:
        to = (flip(mine, bit) * inner + seat, col)
        started = []
        for mask in held:
            for i in range(2):
                place = raws[i].at[flip(mine, mask), seat, :, slab_share(col)]
                k = bit + mask
                started.append(send(place, place, line_send.at[i, k], line_recv.at[i, k], to))
        for copy in started:
            copy.start()
        sent.extend(started)
        held = held + [mask + bit for mask in held]
        if next_part < parts - 1:
            start_waves(next_part)
            next_part += 1
        for copy in started:
            copy.wait_recv()
    groups = []
    for s in range(inner):
        for d in range(col_count):
            if s == 0 and d == 0:
                continue
            to = (mine * inner + lax.rem(seat + s, inner), lax.rem(col + d, col_count))
            for i in range(2):
                place = raws[i].at[:, seat, :, slab_share(col)]
                copy = send(place, place, group_send.at[i, s, d], group_recv.at[i, s, d], to)
                copy.start()
                groups.append(copy)
    while next_part < parts:
        start_waves(next_part)
        next_part += 1

    per_point = points // NC
    fill(swap, lambda p, n: n == (p & (NC - 1)) * per_point + lax.div(p, NC), min(LANES, points))
    if fused:
        per = LANES // NB
        inside = per * NB

        def piece(p, n):
            k, j, w = lax.div(p, inside), lax.div(p & (inside - 1), NB), p & (NB - 1)
            return n == j * inside + k * NB + w

        fill(piece_swap, piece, LANES)
        acc_re[...] = jnp.zeros_like(acc_re)
        acc_im[...] = jnp.zeros_like(acc_im)

    for copy in groups:
        copy.wait_recv()

    for i, decay in enumerate((occ_decay, vir_decay)):
        raw, left = raws[i], lefts[i]
        bands = raw.shape[2]
        join = max(1, LANES // (inner * bands))
        width = join * inner * bands

        def scale(m, carry, raw=raw, left=left, decay=decay, width=width, join=join):
            lanes = pl.ds(pl.multiple_of(m * width, width), width)
            factors = decay[:, lanes]
            for t in range(window // LANES):
                piece = raw[pl.ds(m * join, join), :, :, pl.ds(t * LANES, LANES)]
                turned = piece.reshape(width, LANES).astype(jnp.float32).T * factors
                turned = turned.astype(jnp.bfloat16)
                for s in range(LANES // HALF_ROWS):
                    q = (t * LANES + s * HALF_ROWS) // (HALVES * HALF_ROWS)
                    at = ((s % HALVES) * row_count + q) * HALF_ROWS
                    left[pl.ds(at, HALF_ROWS), lanes] = turned[s * HALF_ROWS : (s + 1) * HALF_ROWS]
            return carry

        lax.fori_loop(0, outer // join, scale, 0)

    def product(h, first, width):
        rows = pl.ds(h * block_rows, block_rows)
        lanes = pl.ds(first, width)
        green = []
        for i in range(2):
            wave = planes[i][:, :, lanes]
            wave = wave.reshape(wave.shape[0] * wave.shape[1], width)
            green.append(dot(lefts[i][rows, :], wave))
        value = (green[0] * green[1] * factor).astype(jnp.bfloat16)
        return dot(value, swap[lanes, :])

    for copy in own[:2]:
        copy.wait()
    for part in range(parts):
        wait_waves(part)
        first, width = cuts[part], cuts[part + 1] - cuts[part]
        for h in range(HALVES):
            moved = product(h, first, width)
            if part:
                moved = mixed[h] + moved
            if part < parts - 1:
                mixed[h] = moved
            else:
                polar[h] = moved.astype(jnp.bfloat16).reshape(row_count, HALF_ROWS, points)
                gives = []
                for k in range(row_count - 1, 0, -1):
                    to = peer(k)
                    copy = send(
                        polar.at[h, to],
                        x_ref.at[h, col, row],
                        give_send.at[h, k],
                        give_recv.at[h, k],
                        (to, col),
                    )
                    copy.start()
                    gives.append(copy)
                if h == 0:
                    early = gives
                else:
                    late = gives
    gives = [list(reversed(early)), list(reversed(late))]

    passes = [[], []]

    def hand_on(h, k, src, slot):
        for d in range(1, col_count):
            to = (row, lax.rem(col + d, col_count))
            copy = send(src, slot, pass_send.at[h, d, k], pass_recv.at[h, d, k], to)
            copy.start()
            passes[h].append((k, copy))

    def forward(h, k):
        gives[h][k - 1].wait_recv()
        slot = x_ref.at[h, col, source(k)]
        hand_on(h, k, slot, slot)

    keep = []
    for h in range(HALVES):
        here = x_ref.at[h, col, row]
        copy = pltpu.make_async_copy(polar.at[h, row], here, local.at[2 + h])
        copy.start()
        keep.append(copy)
        hand_on(h, 0, polar.at[h, row], here)
    near = row_count // 2
    for h in range(HALVES):
        for k in range(1, near):
            forward(h, k)
    for copy in keep:
        copy.wait()

    def wait_pass(h, ks):
        for k, copy in passes[h]:
            if k in ks:
                copy.wait_recv()

    if fused:
        for copy in own[2:]:
            copy.wait()
        per = LANES // NB
        side = lax.div(row, near)
        other = 1 - side

        def transform(h, c, z):
            wide = near * NB
            for g in range(near // per):
                parts = []
                for t in range(NC // per):
                    lanes = pl.ds(t * LANES, LANES)
                    parts.append(
                        jnp.concatenate(
                            [x_ref[h, c, z * near + g * per + k, :, lanes] for k in range(per)], axis=1
                        )
                    )
                moved = dot(jnp.concatenate(parts, axis=0), piece_swap[...]).astype(jnp.bfloat16)
                for t in range(NC // per):
                    for j in range(per):
                        lines_buf[
                            pl.ds((t * per + j) * R_BLOCK, R_BLOCK), pl.ds(g * LANES, LANES)
                        ] = moved[t * R_BLOCK : (t + 1) * R_BLOCK, j * LANES : (j + 1) * LANES]
            line = dot(line_ref[...], lines_buf[...]).astype(jnp.bfloat16)
            half = line.shape[0] // 2
            re, im = line[:half], line[half:]
            depth = pl.ds(pl.multiple_of((c * 2 + z) * wide, wide), wide)
            rows = pl.ds(pl.multiple_of(h * half, half), half)
            cosine, sine = cos_ref[depth, :], sin_ref[depth, :]
            acc_re[rows, :] += dot(re, cosine) + dot(im, sine)
            acc_im[rows, :] += dot(im, cosine) - dot(re, sine)

        def over(jobs):
            def step(i, carry):
                h, c, z = jobs(i)
                transform(h, c, z)
                return carry

            return step

        lax.fori_loop(0, HALVES, over(lambda i: (i, col, side)), 0)
    for k in range(near, row_count):
        forward(0, k)
    for h in range(HALVES):
        wait_pass(h, range(near))
    wait_pass(0, range(near, row_count))
    if fused:
        for d in range(1, col_count):
            there = lax.rem(col + d, col_count)
            lax.fori_loop(0, HALVES, over(lambda i, there=there: (i, there, side)), 0)
        for d in range(col_count):
            transform(0, lax.rem(col + d, col_count), other)
    for k in range(near, row_count):
        forward(1, k)
    if fused:
        transform(1, col, other)
    wait_pass(1, range(near, row_count))
    if fused:
        for d in range(1, col_count):
            transform(1, lax.rem(col + d, col_count), other)

    for _, copy in waiting:
        copy.wait_send()
    for copy in sent + groups + gives[0] + gives[1]:
        copy.wait_send()
    for h in range(HALVES):
        for _, copy in passes[h]:
            copy.wait_send()

    @pl.when(col == 0)
    def _():
        for i in range(2):
            for c in range(1, col_count):
                over_col(i, c).wait_send()

    if not fused:
        for copy in own[2:]:
            copy.wait()


def whole(row_count, col_count, occ, vir, occ_decay, vir_decay, window, factor):
    inner = group_size(row_count)
    outer = row_count // inner
    points = occ.shape[1] // row_count
    fused = points == NB * NC and row_count * col_count == NA and (row_count // 2) % (LANES // NB) == 0
    quarter = points // 4
    cuts = tuple(range(0, points + 1, quarter)) if quarter % LANES == 0 else (0, points)
    parts = len(cuts) - 1
    bands = (occ.shape[0], vir.shape[0])
    block_rows = row_count * HALF_ROWS
    bf16, f32 = jnp.bfloat16, jnp.float32
    dma = pltpu.SemaphoreType.DMA
    vmem = pl.BlockSpec(memory_space=pltpu.VMEM)
    hbm = pl.BlockSpec(memory_space=pltpu.HBM)
    x_shape = (HALVES, col_count, row_count, HALF_ROWS, points)
    operands = [occ, vir, occ_decay, vir_decay]
    in_specs = [hbm, hbm, vmem, vmem]
    scratch = [pltpu.VMEM((row_count, b, points), bf16) for b in bands]
    scratch += [pltpu.VMEM((outer, inner, b, window), bf16) for b in bands]
    scratch += [pltpu.VMEM((window, row_count * b), bf16) for b in bands]
    scratch += [
        pltpu.VMEM((HALVES, block_rows, points), f32),
        pltpu.VMEM((HALVES, row_count, HALF_ROWS, points), bf16),
        pltpu.VMEM((points, points), bf16),
    ]
    if fused:
        cosine, sine = plane_tables()
        line = line_tables(col_count)
        operands += [line, cosine, sine]
        in_specs += [hbm] * 3
        wide = (LANES // NB) * LANES
        scratch += [
            pltpu.VMEM(x_shape, bf16),
            pltpu.VMEM((wide, wide), bf16),
            pltpu.VMEM(line.shape[1:], bf16),
            pltpu.VMEM(cosine.shape, bf16),
            pltpu.VMEM(sine.shape, bf16),
            pltpu.VMEM((NC * R_BLOCK, (row_count // 2) * NB), bf16),
            dma((3,)),
        ]
        out = jax.ShapeDtypeStruct((HALVES * line.shape[1] // 2, NAB), f32)
        out_shape = [out, out]
    else:
        out_shape = [jax.ShapeDtypeStruct(x_shape, bf16)]
    scratch += [dma((2, parts, row_count))] * 2
    scratch += [dma((2, col_count))] * 2
    scratch += [dma((2, outer))] * 2
    scratch += [dma((2, inner, col_count))] * 2
    scratch += [dma((HALVES, row_count))] * 2
    scratch += [dma((HALVES, col_count, row_count))] * 2
    scratch += [dma((4,))]
    cfg = (row_count, col_count, inner, cuts, factor, fused)
    result = pl.pallas_call(
        functools.partial(whole_kernel, cfg),
        out_shape=out_shape,
        in_specs=in_specs,
        out_specs=[vmem] * len(out_shape),
        scratch_shapes=scratch,
        compiler_params=pltpu.CompilerParams(
            collective_id=0, has_side_effects=True, vmem_limit_bytes=52 * 1024 * 1024
        ),
    )(*operands)
    return fused, result


def on_device(rows_dev, occupied_waves, virtual_waves, occupied_decay, virtual_decay):
    row_count = lax.axis_size("row")
    col_count = lax.axis_size("col")
    nocc, nvir = occupied_decay.shape[0], virtual_decay.shape[0]
    window = rows_dev * row_count
    points = occupied_waves.shape[1] // row_count
    factor = -1.0 / math.sqrt(nocc * nvir) / math.sqrt(NGRID)
    fused, result = whole(
        row_count,
        col_count,
        occupied_waves,
        virtual_waves,
        occupied_decay.reshape(1, nocc),
        virtual_decay.reshape(1, nvir),
        window,
        factor,
    )
    if fused:
        real_part, imag_part = result
    else:
        x = result[0].reshape(HALVES, col_count * row_count, R_BLOCK, NC, points // NC)
        x = jnp.transpose(x, (3, 0, 2, 1, 4)).reshape(NC, rows_dev, NAB)
        real_part, imag_part = spectrum(x, line_tables(col_count))
    shape = (rows_dev, NC // col_count, NAB)
    return real_part.reshape(shape), imag_part.reshape(shape)


ROWS_DEV = 32


def solution(mesh):
    in_specs = (P("row", "col"), P("row", "col"), P(), P())
    out_specs = (P("row", "col", None), P("row", "col", None))
    return jax.shard_map(
        functools.partial(on_device, ROWS_DEV),
        mesh=mesh,
        in_specs=in_specs,
        out_specs=out_specs,
        check_vma=False,
    )
```

time: 139 us -> 134 us (0.964)
  the two profiles are of different devices: /device:TPU:0 before, /device:TPU:12 now
where the time goes in v1:
time: 134 us
  Pallas kernels  126 us (94%)
  local copies, waits for them, and re-layouts  7.22 us (5%)
    pallas_call x1, Pallas kernels, whole(): pl.pallas_call(functools.partial(whole_kernel, cfg), out_shape=out_shape,...  126 us
    unnamed x10, local copies, waits for them, and re-layouts  7.22 us

profile of v1, /device:TPU:12, one launch (start us, length us, event | category | flops | bytes accessed | tf_op | source)
XLA Modules:
  0.0 134.0 jit_solution(5554279512765977963)
XLA Ops:
  0.6 0.0 copy-start
  0.6 1.2 copy-done
  1.9 0.0 copy-start.1
  1.9 0.7 copy-done.1
  2.5 0.0 copy-start.2
  2.5 0.7 copy-done.2
  3.2 126.1 %shard_map.86 = (f32[512,1024]{1,0:T(8,128)}, f32[512,1024]{1,0:T(8,128)}) custom-call(bf16[64,16384]{1,0:T(8,128)(2,1)} %refs_0_.1, bf16[32,16384]{1,0:T(8,128)(2,1)S(1)} %copy-done, f32[1,1024]{1,0:T(1,128)S(1)} %bitcast.4, f32[1,512]{1,0:T(1,128)S(1)} %bitcast.5, bf16[2,512,512]{2,1,0:T(8,128)(2,1)} %constant.9.refs_4_, ...), custom_call_target="tpu_custom_call" | custom-call | tf_op jit(solution)/shard_map/pallas_call | solution.py:533
  129.4 0.0 copy-start.3
  129.4 3.3 %copy.11 = f32[32,16,1024]{2,1,0:T(8,128)} copy(f32[32,16,1024]{2,1,0:T(8,128)} %bitcast.7) | data formatting | bytes 4194304
  132.7 0.0 copy-done.3
  132.7 1.3 copy.12
Async XLA Ops:
  0.6 1.2 copy-start
  1.9 0.7 copy-start.1
  2.5 0.7 copy-start.2
  129.4 3.3 %copy-start.3 = (f32[512,1024]{1,0:T(8,128)S(1)}, f32[512,1024]{1,0:T(8,128)}, u32[]{:S(2)}) copy-start(f32[512,1024]{1,0:T(8,128)} %get-tuple-element.5) | copy-start | bytes 6291460

commit v2 on v1

v2 whole, which is shorter than its diff:
```python
import functools
import math

import jax
import jax.numpy as jnp
import numpy as np
from jax import lax
from jax.experimental import pallas as pl
from jax.experimental.pallas import tpu as pltpu
from jax.sharding import PartitionSpec as P

NA = 32
NB = 32
NC = 32
NAB = NA * NB
NGRID = NA * NB * NC
LANES = 128
R_BLOCK = 16


def trig(phase, length):
    angle = (phase % length) * (2.0 * math.pi / length)
    return np.cos(angle), np.sin(angle)


def bf16_table(table):
    return jnp.asarray(table.astype(np.float32)).astype(jnp.bfloat16)


def plane_tables():
    index = np.arange(NAB)
    a, b = index // NB, index % NB
    phase = a[:, None] * a[None, :] * NB + b[:, None] * b[None, :] * NA
    cosine, sine = trig(phase, NA * NB)
    return bf16_table(cosine), bf16_table(sine)


def line_tables(col_count):
    share = NC // col_count
    full = np.zeros((col_count, 2, R_BLOCK, share, NC, R_BLOCK))
    for y in range(col_count):
        kc = y * share + np.arange(share)
        cosine, sine = trig(kc[:, None] * np.arange(NC)[None, :], NC)
        for r in range(R_BLOCK):
            full[y, 0, r, :, :, r] = cosine
            full[y, 1, r, :, :, r] = -sine
    return bf16_table(full.reshape(col_count, 2 * R_BLOCK * share, NC * R_BLOCK))


def dot(a, b):
    return jnp.dot(a, b, preferred_element_type=jnp.float32)


def spectrum_kernel(x_ref, line_ref, cos_ref, sin_ref, re_ref, im_ref):
    rows = x_ref[...].reshape(NC * R_BLOCK, NAB)
    line = dot(line_ref[lax.axis_index("col")], rows).astype(jnp.bfloat16)
    half = line.shape[0] // 2
    re, im = line[:half], line[half:]
    re_ref[...] = dot(re, cos_ref[...]) + dot(im, sin_ref[...])
    im_ref[...] = dot(im, cos_ref[...]) - dot(re, sin_ref[...])


def spectrum(x, line_table):
    r_count = x.shape[1]
    cosine, sine = plane_tables()
    out_rows = line_table.shape[1] // 2
    steps = r_count // R_BLOCK
    whole = lambda table: pl.BlockSpec(table.shape, lambda i: (0,) * table.ndim)
    out = jax.ShapeDtypeStruct((out_rows * steps, NAB), jnp.float32)
    out_spec = pl.BlockSpec((out_rows, NAB), lambda i: (i, 0))
    return pl.pallas_call(
        spectrum_kernel,
        grid=(steps,),
        in_specs=[
            pl.BlockSpec((x.shape[0], R_BLOCK, x.shape[2]), lambda i: (0, i, 0)),
            whole(line_table),
            whole(cosine),
            whole(sine),
        ],
        out_specs=[out_spec, out_spec],
        out_shape=[out, out],
        compiler_params=pltpu.CompilerParams(vmem_limit_bytes=48 * 1024 * 1024),
    )(x, line_table, cosine, sine)


MESH = pl.DeviceIdType.MESH
HALVES = 2
VMEM_LIMIT = 47 * 1024 * 1024
PIECES = 4
FARS = 4
HALF_ROWS = R_BLOCK


def flip(index, mask):
    bits = [1 << bit for bit in range(mask.bit_length()) if mask >> bit & 1]
    for bit in bits:
        index = index + bit - 2 * bit * lax.rem(lax.div(index, bit), 2)
    return index


def group_size(row_count):
    return 4 if row_count % 4 == 0 else 1


def send(src, dst, send_sem, recv_sem, target):
    return pltpu.make_async_remote_copy(
        src_ref=src,
        dst_ref=dst,
        send_sem=send_sem,
        recv_sem=recv_sem,
        device_id=target,
        device_id_type=MESH,
    )


def drain(ref, sem):
    pltpu.make_async_copy(ref, ref, sem).wait()


def enter(row_count, col_count, inner, row, col):
    barrier = pltpu.get_barrier_semaphore()
    targets = [(flip(row, k), col) for k in range(1, row_count)]
    targets += [
        (flip(row, s), lax.rem(col + d, col_count))
        for d in range(1, col_count)
        for s in range(inner)
    ]
    for target in targets:
        pl.semaphore_signal(barrier, inc=1, device_id=target, device_id_type=MESH)
    return barrier, len(targets)


def fill(ref, values, rows):
    width = ref.shape[1]

    def step(i, carry):
        start = pl.multiple_of(i * rows, rows)
        row = lax.broadcasted_iota(jnp.int32, (rows, width), 0) + start
        lane = lax.broadcasted_iota(jnp.int32, (rows, width), 1)
        ref[pl.ds(start, rows), :] = jnp.where(values(row, lane), 1.0, 0.0).astype(jnp.bfloat16)
        return carry

    lax.fori_loop(0, ref.shape[0] // rows, step, 0)


def spread(blocks, swap, lines_buf, line_table):
    per = LANES // NB
    for g in range(len(blocks) // per):
        pieces = []
        for t in range(NC // per):
            lanes = pl.ds(t * LANES, LANES)
            pieces.append(jnp.concatenate([blocks[g * per + k][:, lanes] for k in range(per)], axis=1))
        moved = dot(jnp.concatenate(pieces, axis=0), swap[...]).astype(jnp.bfloat16)
        for t in range(NC // per):
            for j in range(per):
                lines_buf[pl.ds((t * per + j) * R_BLOCK, R_BLOCK), pl.ds(g * LANES, LANES)] = moved[
                    t * R_BLOCK : (t + 1) * R_BLOCK, j * LANES : (j + 1) * LANES
                ]
    line = dot(line_table[...], lines_buf[...]).astype(jnp.bfloat16)
    half = line.shape[0] // 2
    return line[:half], line[half:]


def whole_kernel(cfg, *refs):
    (row_count, col_count, inner, cuts, factor, fused) = cfg
    refs = list(refs)
    take = lambda n: [refs.pop(0) for _ in range(n)]
    occ_ref, vir_ref, occ_decay, vir_decay = take(4)
    if fused:
        (table_hbm,) = take(1)
        parts_out = take(2 * PIECES)
        tail_x, tail_cos, tail_sin, tail_line, tail_swap = take(5)
    else:
        (x_ref,) = take(1)
    planes = take(2)
    raws = take(2)
    lefts = take(2)
    mixed, polar, swap = take(3)
    if fused:
        x_ref, piece_swap, line_ref, cos_ref, sin_ref, lines_buf, acc_re, acc_im = take(8)
        table_sem, out_sem, tail_sem = take(3)
    (wave_send, wave_recv, col_send, col_recv, line_send, line_recv, share_send, share_recv) = take(8)
    (give_send, give_recv, pass_send, pass_recv, local) = take(5)

    row, col = lax.axis_index("row"), lax.axis_index("col")
    outer = row_count // inner
    mine, seat = lax.div(row, inner), lax.rem(row, inner)
    points = occ_ref.shape[1] // row_count
    waves = (occ_ref, vir_ref)
    window = raws[0].shape[3]
    share = window // col_count
    block_rows = row_count * HALF_ROWS

    def peer(k):
        return flip(row, k)

    barrier, arrivals = enter(row_count, col_count, inner, row, col)

    own = []
    for i in range(2):
        lanes = pl.ds(pl.multiple_of(row * points, LANES), points)
        own.append(pltpu.make_async_copy(waves[i].at[:, lanes], planes[i].at[row], local.at[i]))
    if fused:
        width = line_ref.shape[0]
        lines = pl.ds(pl.multiple_of(2 * NAB + col * width, width), width)
        own.append(pltpu.make_async_copy(table_hbm.at[lines, pl.ds(0, width)], line_ref, table_sem.at[0]))
        own.append(pltpu.make_async_copy(table_hbm.at[pl.ds(0, NAB)], cos_ref, table_sem.at[1]))
        own.append(pltpu.make_async_copy(table_hbm.at[pl.ds(NAB, NAB)], sin_ref, table_sem.at[2]))
    for copy in own:
        copy.start()
    pl.semaphore_wait(barrier, arrivals)

    def start_waves(part, ks):
        first, last = cuts[part], cuts[part + 1]
        for k in ks:
            to = peer(k)
            lanes = pl.ds(pl.multiple_of(to * points + first, LANES), last - first)
            for i in range(2):
                copy = send(
                    waves[i].at[:, lanes],
                    planes[i].at[row, :, pl.ds(first, last - first)],
                    wave_send.at[i],
                    wave_recv.at[i, part],
                    (to, col),
                )
                copy.start()

    def wait_waves(part):
        lanes = pl.ds(cuts[part], cuts[part + 1] - cuts[part])
        for i in range(2):
            drain(planes[i].at[pl.ds(0, row_count - 1), :, lanes], wave_recv.at[i, part])

    parts = len(cuts) - 1
    near = row_count // 2

    def slab_share(c):
        return pl.ds(c * share, share) if isinstance(c, int) else pl.ds(pl.multiple_of(c * share, LANES), share)

    def over_col(i, c):
        return send(
            waves[i].at[:, slab_share(c)],
            raws[i].at[mine, seat, :, slab_share(c)],
            col_send.at[i, c - 1],
            col_recv.at[i],
            (row, c),
        )

    @pl.when(col == 0)
    def _():
        for i in range(2):
            for c in range(1, col_count):
                over_col(i, c).start()
            pltpu.make_async_copy(
                waves[i].at[:, slab_share(0)], raws[i].at[mine, seat, :, slab_share(0)], local.at[2 + i]
            ).start()

    far = range(near, row_count)
    queue = [k for s in range(inner) for k in far if k % inner == s]
    queue += [k for k in range(inner, near)] + [k for k in range(1, inner)]

    def advance(count):
        start_waves(0, queue[:count])
        del queue[:count]

    advance(1)

    @pl.when(col == 0)
    def _():
        for i in range(2):
            pltpu.make_async_copy(
                waves[i].at[:, slab_share(0)], raws[i].at[mine, seat, :, slab_share(0)], local.at[2 + i]
            ).wait()

    if col_count > 1:

        @pl.when(col != 0)
        def _():
            for i in range(2):
                over_col(i, 1).wait_recv()

    sent = []
    mine, seat = lax.div(row, inner), lax.rem(row, inner)

    def exchange(pairs):
        started = [send(place, place, line_send.at[i, n], line_recv.at[i, n], to) for i, n, place, to in pairs]
        for copy in started:
            copy.start()
        sent.extend(started)
        return started

    held = [0]
    number = 0
    for bit in [1 << bit for bit in reversed(range((outer - 1).bit_length()))]:
        to = (flip(row, bit * inner), col)
        started = exchange(
            [
                (i, number + n, raws[i].at[flip(mine, mask), seat, :, slab_share(col)], to)
                for n, mask in enumerate(held)
                for i in range(2)
            ]
        )
        number += len(held)
        held = held + [mask + bit for mask in held]
        advance(1)
        for copy in started:
            copy.wait_recv()
    started = []
    for d in range(1, col_count):
        for i in range(2):
            place = raws[i].at[:, seat, :, slab_share(col)]
            to = (row, lax.rem(col + d, col_count))
            started.append(send(place, place, share_send.at[i, d - 1], share_recv.at[i, d - 1], to))
    for copy in started:
        copy.start()
    sent.extend(started)
    advance(1)
    for copy in started:
        copy.wait_recv()
    held = [0]
    for bit in [1 << bit for bit in reversed(range((inner - 1).bit_length()))]:
        to = (flip(row, bit), col)
        started = exchange(
            [
                (i, number + n, raws[i].at[:, flip(seat, mask)], to)
                for n, mask in enumerate(held)
                for i in range(2)
            ]
        )
        number += len(held)
        held = held + [mask + bit for mask in held]
        advance(2)
        for copy in started:
            copy.wait_recv()
    advance(len(queue))
    order = [k for k in far] + [k for k in range(inner, near)] + [k for k in range(1, inner)]
    for part in range(1, parts):
        start_waves(part, order)

    per_point = points // NC
    fill(swap, lambda p, n: n == (p & (NC - 1)) * per_point + lax.div(p, NC), min(LANES, points))
    if fused:
        per = LANES // NB
        inside = per * NB

        def piece(p, n):
            k, j, w = lax.div(p, inside), lax.div(p & (inside - 1), NB), p & (NB - 1)
            return n == j * inside + k * NB + w

        fill(piece_swap, piece, LANES)
        acc_re[...] = jnp.zeros_like(acc_re)
        acc_im[...] = jnp.zeros_like(acc_im)

    for i, decay in enumerate((occ_decay, vir_decay)):
        raw, left = raws[i], lefts[i]
        bands = raw.shape[2]
        join = max(1, LANES // (inner * bands))
        width = join * inner * bands

        def scale(m, carry, raw=raw, left=left, decay=decay, width=width, join=join):
            lanes = pl.ds(pl.multiple_of(m * width, width), width)
            factors = decay[:, lanes]
            for t in range(window // LANES):
                piece = raw[pl.ds(m * join, join), :, :, pl.ds(t * LANES, LANES)]
                turned = piece.reshape(width, LANES).astype(jnp.float32).T * factors
                turned = turned.astype(jnp.bfloat16)
                for s in range(LANES // HALF_ROWS):
                    q = (t * LANES + s * HALF_ROWS) // (HALVES * HALF_ROWS)
                    at = ((s % HALVES) * row_count + q) * HALF_ROWS
                    left[pl.ds(at, HALF_ROWS), lanes] = turned[s * HALF_ROWS : (s + 1) * HALF_ROWS]
            return carry

        lax.fori_loop(0, outer // join, scale, 0)

    def product(h, first, width):
        rows = pl.ds(h * block_rows, block_rows)
        lanes = pl.ds(first, width)
        green = []
        for i in range(2):
            wave = planes[i][:, :, lanes]
            wave = wave.reshape(wave.shape[0] * wave.shape[1], width)
            green.append(dot(lefts[i][rows, :], wave))
        value = (green[0] * green[1] * factor).astype(jnp.bfloat16)
        return dot(value, swap[lanes, :])

    for copy in own[:2]:
        copy.wait()
    ordered = [k for s in range(inner) for k in far if k % inner == s]
    quarter = len(ordered) // FARS
    fars = [ordered[n * quarter : (n + 1) * quarter] for n in range(FARS)]
    keep = []

    def to_row(h, ks, group):
        for k in ks:
            send(
                polar.at[h, peer(k)],
                x_ref.at[h, col, row],
                give_send.at[h],
                give_recv.at[h, group],
                (peer(k), col),
            ).start()

    def to_cols(h, ks):
        for k in ks:
            for d in range(1, col_count):
                send(
                    polar.at[h, peer(k)],
                    x_ref.at[h, col, row],
                    pass_send.at[h],
                    pass_recv.at[h, d - 1, 0],
                    (peer(k), lax.rem(col + d, col_count)),
                ).start()

    def forward(h, group):
        some = fars[group]
        drain(x_ref.at[h, col, pl.ds(0, len(some))], give_recv.at[h, 1 + group])
        for k in some:
            arrived = x_ref.at[h, col, peer(k)]
            for d in range(1, col_count):
                slot = arrived
                if fused and h == HALVES - 1:
                    slot = tail_x.at[d - 1, lax.rem(peer(k), near)]
                to = (row, lax.rem(col + d, col_count))
                send(arrived, slot, pass_send.at[h], pass_recv.at[h, d - 1, 1], to).start()

    def wait_near(h):
        drain(x_ref.at[h, col, pl.ds(0, near - 1)], give_recv.at[h, 0])
        keep[h].wait()

    def wait_pass(h, which):
        for d in range(1, col_count):
            count = row_count - near if which else near
            drain(x_ref.at[h, col, pl.ds(0, count)], pass_recv.at[h, d - 1, which])

    def give(h):
        copy = pltpu.make_async_copy(polar.at[h, row], x_ref.at[h, col, row], local.at[2 + h])
        copy.start()
        keep.append(copy)
        to_cols(h, range(min(2, inner)))
        for group in range(FARS):
            to_row(h, fars[group], 1 + group)
        to_row(h, range(inner, near), 0)
        to_row(h, range(1, inner), 0)
        to_cols(h, range(min(2, inner), near))

    for part in range(parts):
        wait_waves(part)
        first, last = cuts[part], cuts[part + 1]
        tile = min(last - first, 2 * LANES)
        for h in range(HALVES):
            moved = mixed[h] if part else None
            for start in range(first, last, tile):
                term = product(h, start, tile)
                moved = term if moved is None else moved + term
            if part < parts - 1:
                mixed[h] = moved
            else:
                polar[h] = moved.astype(jnp.bfloat16).reshape(row_count, HALF_ROWS, points)
                give(h)

    if fused:
        for copy in own[2:]:
            copy.wait()
        per = LANES // NB
        side = lax.div(row, near)
        other = 1 - side

        wide = near * NB
        tails = [
            pltpu.make_async_copy(line_ref, tail_line, tail_sem.at[0]),
            pltpu.make_async_copy(piece_swap, tail_swap, tail_sem.at[1]),
        ]
        for d in range(1, col_count):
            c = lax.rem(col + col_count - d, col_count)
            depth = pl.ds(pl.multiple_of((c * 2 + other) * wide, wide), wide)
            tails.append(pltpu.make_async_copy(cos_ref.at[depth], tail_cos.at[d - 1], tail_sem.at[2 * d]))
            tails.append(pltpu.make_async_copy(sin_ref.at[depth], tail_sin.at[d - 1], tail_sem.at[2 * d + 1]))
        for copy in tails:
            copy.start()

        def transform(h, c, z):
            blocks = [x_ref.at[h, c, z * near + a] for a in range(near)]
            re, im = spread(blocks, piece_swap, lines_buf, line_ref)
            depth = pl.ds(pl.multiple_of((c * 2 + z) * wide, wide), wide)
            cosine, sine = cos_ref[depth, :], sin_ref[depth, :]
            acc_re[h] += dot(re, cosine) + dot(im, sine)
            acc_im[h] += dot(im, cosine) - dot(re, sine)

        def put_out(h):
            per_half = PIECES // HALVES
            height = acc_re.shape[1] // per_half
            for i, acc in enumerate((acc_re, acc_im)):
                for n in range(per_half):
                    p = i * PIECES + h * per_half + n
                    pltpu.make_async_copy(
                        acc.at[h, pl.ds(n * height, height)], parts_out[p], out_sem.at[h]
                    ).start()

    else:
        side = other = 0

        def transform(h, c, z):
            return

        def put_out(h):
            return

        tails = []
    others = [lax.rem(col + d, col_count) for d in range(1, col_count)]
    forward(0, 0)
    forward(0, 1)
    wait_near(0)
    transform(0, col, side)
    forward(0, 2)
    forward(0, 3)
    wait_pass(0, 0)
    for c in others:
        transform(0, c, side)
    transform(0, col, other)
    forward(1, 0)
    forward(1, 1)
    wait_near(1)
    transform(1, col, side)
    forward(1, 2)
    wait_pass(0, 1)
    for c in others:
        transform(0, c, other)
    put_out(0)
    wait_pass(1, 0)
    for c in others:
        transform(1, c, side)
    forward(1, 3)
    transform(1, col, other)
    put_out(1)
    wait_pass(1, 1)
    for copy in tails:
        copy.wait()
    if fused:
        for h in range(HALVES):
            drain(acc_re, out_sem.at[h])

    for i in range(2):
        drain(planes[i].at[pl.ds(0, row_count - 1)], wave_send.at[i])
    for copy in sent:
        copy.wait_send()
    for h in range(HALVES):
        drain(x_ref.at[h, col, pl.ds(0, row_count - 1)], give_send.at[h])
        for d in range(1, col_count):
            drain(x_ref.at[h, col], pass_send.at[h])

    @pl.when(col == 0)
    def _():
        for i in range(2):
            for c in range(1, col_count):
                over_col(i, c).wait_send()

    if not fused:
        for copy in own[2:]:
            copy.wait()


def whole(row_count, col_count, occ, vir, occ_decay, vir_decay, window, factor):
    inner = group_size(row_count)
    outer = row_count // inner
    points = occ.shape[1] // row_count
    fused = points == NB * NC and row_count * col_count == NA and (row_count // 2) % (LANES // NB) == 0
    quarter = points // 4
    cuts = (0, points - quarter, points) if quarter % LANES == 0 else (0, points)
    parts = len(cuts) - 1
    bands = (occ.shape[0], vir.shape[0])
    block_rows = row_count * HALF_ROWS
    bf16, f32 = jnp.bfloat16, jnp.float32
    dma = pltpu.SemaphoreType.DMA
    vmem = pl.BlockSpec(memory_space=pltpu.VMEM)
    hbm = pl.BlockSpec(memory_space=pltpu.HBM)
    x_shape = (HALVES, col_count, row_count, HALF_ROWS, points)
    operands = [occ, vir, occ_decay, vir_decay]
    in_specs = [hbm, hbm, vmem, vmem]
    scratch = [pltpu.VMEM((row_count, b, points), bf16) for b in bands]
    scratch += [pltpu.VMEM((outer, inner, b, window), bf16) for b in bands]
    scratch += [pltpu.VMEM((window, row_count * b), bf16) for b in bands]
    scratch += [
        pltpu.VMEM((HALVES, block_rows, points), f32),
        pltpu.VMEM((HALVES, row_count, HALF_ROWS, points), bf16),
        pltpu.VMEM((points, points), bf16),
    ]
    if fused:
        cosine, sine = plane_tables()
        line = line_tables(col_count)
        flat = jnp.pad(line.reshape(-1, line.shape[2]), ((0, 0), (0, NAB - line.shape[2])))
        operands += [jnp.concatenate([cosine, sine, flat])]
        in_specs += [hbm]
        wide = (LANES // NB) * LANES
        scratch += [
            pltpu.VMEM(x_shape, bf16),
            pltpu.VMEM((wide, wide), bf16),
            pltpu.VMEM(line.shape[1:], bf16),
            pltpu.VMEM(cosine.shape, bf16),
            pltpu.VMEM(sine.shape, bf16),
            pltpu.VMEM((NC * R_BLOCK, (row_count // 2) * NB), bf16),
        ]
        scratch += [pltpu.VMEM((HALVES, line.shape[1] // 2, NAB), f32)] * 2
        scratch += [dma((3,)), dma((HALVES,)), dma((2 * col_count,))]
        out_shape = [jax.ShapeDtypeStruct((HALVES * line.shape[1] // 2 // PIECES, NAB), f32)] * (2 * PIECES)
        late = col_count - 1
        near = row_count // 2
        tails = [(late, near, HALF_ROWS, points)] + [(late, near * NB, NAB)] * 2 + [line.shape[1:], (wide, wide)]
        out_shape += [jax.ShapeDtypeStruct(shape, bf16) for shape in tails]
    else:
        out_shape = [jax.ShapeDtypeStruct(x_shape, bf16)]
    places = max(1, col_count - 1)
    steps = outer - 1 + inner - 1
    scratch += [dma((2,)), dma((2, parts)), dma((2, places)), dma((2,))]
    scratch += [dma((2, steps))] * 2 + [dma((2, places))] * 2
    scratch += [dma((HALVES,)), dma((HALVES, 1 + FARS)), dma((HALVES,)), dma((HALVES, places, 2))]
    scratch += [dma((4,))]
    cfg = (row_count, col_count, inner, cuts, factor, fused)
    result = pl.pallas_call(
        functools.partial(whole_kernel, cfg),
        out_shape=out_shape,
        in_specs=in_specs,
        out_specs=[pl.BlockSpec(memory_space=pl.ANY) if fused else vmem] * len(out_shape),
        scratch_shapes=scratch,
        compiler_params=pltpu.CompilerParams(
            collective_id=0, has_side_effects=True, vmem_limit_bytes=VMEM_LIMIT
        ),
    )(*operands)
    return fused, result


def last_kernel(*refs):
    parts = refs[: 2 * PIECES]
    tail_x, tail_cos, tail_sin, tail_line, tail_swap, re_out, im_out, lines_buf, *acc, sems = refs[2 * PIECES :]
    outs = (re_out, im_out)
    half = PIECES // HALVES
    rows = parts[0].shape[0]
    copies = []

    def put(i, p, src):
        copy = pltpu.make_async_copy(src, outs[i].at[pl.ds(p * rows, rows)], sems.at[i, p])
        copy.start()
        copies.append(copy)

    for i in range(2):
        for p in range(half):
            put(i, p, parts[i * PIECES + p])
    late = []
    for d in range(tail_x.shape[0]):
        blocks = [tail_x.at[d, a] for a in range(tail_x.shape[1])]
        re, im = spread(blocks, tail_swap, lines_buf, tail_line)
        late.append((re, im, tail_cos[d], tail_sin[d]))
    for n in range(half):
        p = half + n
        at = slice(n * rows, (n + 1) * rows)
        for i in range(2):
            total = parts[i * PIECES + p][...]
            for re, im, cosine, sine in late:
                if i == 0:
                    total = total + (dot(re[at], cosine) + dot(im[at], sine))
                else:
                    total = total + (dot(im[at], cosine) - dot(re[at], sine))
            acc[i][pl.ds(n * rows, rows), :] = total
            put(i, p, acc[i].at[pl.ds(n * rows, rows)])
    for copy in copies:
        copy.wait()


def last(operands):
    rows, lanes = operands[0].shape
    vmem = pl.BlockSpec(memory_space=pltpu.VMEM)
    tail_x = operands[2 * PIECES]
    acc = pltpu.VMEM((rows * PIECES // HALVES, lanes), jnp.float32)
    return pl.pallas_call(
        last_kernel,
        out_shape=[jax.ShapeDtypeStruct((rows * PIECES, lanes), jnp.float32)] * 2,
        in_specs=[vmem] * len(operands),
        out_specs=[pl.BlockSpec(memory_space=pltpu.HBM)] * 2,
        scratch_shapes=[
            pltpu.VMEM((NC * R_BLOCK, tail_x.shape[1] * NB), jnp.bfloat16),
            acc,
            acc,
            pltpu.SemaphoreType.DMA((2, PIECES)),
        ],
        compiler_params=pltpu.CompilerParams(vmem_limit_bytes=8 * 1024 * 1024),
    )(*operands)


def on_device(rows_dev, occupied_waves, virtual_waves, occupied_decay, virtual_decay):
    row_count = lax.axis_size("row")
    col_count = lax.axis_size("col")
    nocc, nvir = occupied_decay.shape[0], virtual_decay.shape[0]
    window = rows_dev * row_count
    points = occupied_waves.shape[1] // row_count
    factor = -1.0 / math.sqrt(nocc * nvir) / math.sqrt(NGRID)
    fused, result = whole(
        row_count,
        col_count,
        occupied_waves,
        virtual_waves,
        occupied_decay.reshape(1, nocc),
        virtual_decay.reshape(1, nvir),
        window,
        factor,
    )
    if fused:
        real_part, imag_part = last(result)
    else:
        x = result[0].reshape(HALVES, col_count * row_count, R_BLOCK, NC, points // NC)
        x = jnp.transpose(x, (3, 0, 2, 1, 4)).reshape(NC, rows_dev, NAB)
        real_part, imag_part = spectrum(x, line_tables(col_count))
    shape = (rows_dev, NC // col_count, NAB)
    return real_part.reshape(shape), imag_part.reshape(shape)


ROWS_DEV = 32


def solution(mesh):
    in_specs = (P("row", "col"), P("row", "col"), P(), P())
    out_specs = (P("row", "col", None), P("row", "col", None))
    return jax.shard_map(
        functools.partial(on_device, ROWS_DEV),
        mesh=mesh,
        in_specs=in_specs,
        out_specs=out_specs,
        check_vma=False,
    )
```

time: 134 us -> 115 us (0.86)
  the two profiles are of different devices: /device:TPU:12 before, /device:TPU:0 now
where the time goes in v2:
time: 115 us; the launch traced here: 114 us
  Pallas kernels  112 us (97%)
  local copies, waits for them, and re-layouts  1.36 us (1%)
    pallas_call x1, Pallas kernels, whole(): pl.pallas_call(functools.partial(whole_kernel, cfg), out_shape=out_shape,...  109 us
    pallas_call x1, Pallas kernels, last(): pl.pallas_call(last_kernel, out_shape=[jax.ShapeDtypeStruct((rows * PIECE...  2.82 us

profile of v2, /device:TPU:0, one launch (start us, length us, event | category | flops | bytes accessed | tf_op | source)
XLA Modules:
  0.0 114.4 jit_solution(10335440793860770867)
XLA Ops:
  0.6 0.0 copy-start
  0.6 0.7 copy-done
  1.3 0.0 copy-start.1
  1.3 0.7 copy-done.1
  2.0 109.4 %shard_map.86 = (f32[128,1024]{1,0:T(8,128)S(1)}, f32[128,1024]{1,0:T(8,128)S(1)}, f32[128,1024]{1,0:T(8,128)S(1)}, f32[128,1024]{1,0:T(8,128)S(1)}, f32[128,102...) custom-call(bf16[64,16384]{1,0:T(8,128)(2,1)} %refs_0_.1, ...), custom_call_target="tpu_custom_call" | custom-call | tf_op jit(solution)/shard_map/pallas_call | solution.py:617
  111.5 2.8 %shard_map.87 = (f32[512,1024]{1,0:T(8,128)}, f32[512,1024]{1,0:T(8,128)}) custom-call(f32[128,1024]{1,0:T(8,128)S(1)} %get-tuple-element.17.refs_0_, f32[128,1024]{1,0:T(8,128)S(1)} %get-tuple-element.18.refs_1_, f32[128,1024]{1,0:T(8,128)S(1)} %get-tuple-element.19.refs_2_, f32[128,1024]{1,0:T(8,128)S(1)} %get-tuple-element.20.refs_3_, ...), custom_call_target="tpu_custom_call" | custom-call | tf_op jit(solution)/shard_map/pallas_call | solution.py:672
Async XLA Ops:
  0.6 0.7 copy-start
  1.3 0.7 copy-start.1

commit v3 on v2

--- a/solution.py
+++ b/solution.py
@@ -27,11 +27,12 @@
     return jnp.asarray(table.astype(np.float32)).astype(jnp.bfloat16)
 
 
-def plane_tables():
+def plane_tables(turns, group):
     index = np.arange(NAB)
     a, b = index // NB, index % NB
     phase = a[:, None] * a[None, :] * NB + b[:, None] * b[None, :] * NA
-    cosine, sine = trig(phase, NA * NB)
+    rows = index.reshape(-1, group // turns, turns, NB).transpose(0, 2, 1, 3).reshape(-1)
+    cosine, sine = trig(phase[rows], NA * NB)
     return bf16_table(cosine), bf16_table(sine)
 
 
@@ -62,7 +63,7 @@
 
 def spectrum(x, line_table):
     r_count = x.shape[1]
-    cosine, sine = plane_tables()
+    cosine, sine = plane_tables(1, NA)
     out_rows = line_table.shape[1] // 2
     steps = r_count // R_BLOCK
     whole = lambda table: pl.BlockSpec(table.shape, lambda i: (0,) * table.ndim)
@@ -85,9 +86,10 @@
 
 MESH = pl.DeviceIdType.MESH
 HALVES = 2
-VMEM_LIMIT = 47 * 1024 * 1024
+VMEM_LIMIT = 48 * 1024 * 1024
 PIECES = 4
 FARS = 4
+AHEAD = (1, 2, 1)
 HALF_ROWS = R_BLOCK
 
 
@@ -143,33 +145,47 @@
     lax.fori_loop(0, ref.shape[0] // rows, step, 0)
 
 
-def spread(blocks, swap, lines_buf, line_table):
-    per = LANES // NB
-    for g in range(len(blocks) // per):
-        pieces = []
-        for t in range(NC // per):
-            lanes = pl.ds(t * LANES, LANES)
-            pieces.append(jnp.concatenate([blocks[g * per + k][:, lanes] for k in range(per)], axis=1))
-        moved = dot(jnp.concatenate(pieces, axis=0), swap[...]).astype(jnp.bfloat16)
-        for t in range(NC // per):
+def spread(blocks, lines_buf, line_table):
+    short = blocks[0].shape[1] // NC
+    per = LANES // short
+    count = blocks[0].shape[1] // LANES
+    groups = len(blocks) // per
+    pieces = []
+    for k in range(per):
+        parts = [blocks[g * per + k][:, pl.ds(t * LANES, LANES)] for g in range(groups) for t in range(count)]
+        pieces.append(jnp.concatenate(parts, axis=0))
+    lane = lax.broadcasted_iota(jnp.int32, pieces[0].shape, 1)
+    bit = per // 2
+    while bit:
+        high = (lane & (bit * short)) != 0
+        for k in range(per):
+            if k & bit:
+                continue
+            a, b = pieces[k], pieces[k + bit]
+            pieces[k] = jnp.where(high, pltpu.roll(b, bit * short, 1), a)
+            pieces[k + bit] = jnp.where(high, b, pltpu.roll(a, LANES - bit * short, 1))
+        bit //= 2
+    for g in range(groups):
+        for t in range(count):
+            at = (g * count + t) * R_BLOCK
             for j in range(per):
-                lines_buf[pl.ds((t * per + j) * R_BLOCK, R_BLOCK), pl.ds(g * LANES, LANES)] = moved[
-                    t * R_BLOCK : (t + 1) * R_BLOCK, j * LANES : (j + 1) * LANES
-                ]
+                place = pl.ds((t * per + j) * R_BLOCK, R_BLOCK)
+                lines_buf[place, pl.ds(g * LANES, LANES)] = pieces[j][at : at + R_BLOCK]
     line = dot(line_table[...], lines_buf[...]).astype(jnp.bfloat16)
     half = line.shape[0] // 2
-    return line[:half], line[half:]
+    re, im = line[:half], line[half:]
+    return jnp.concatenate([jnp.concatenate([re, im], axis=1), jnp.concatenate([im, -re], axis=1)], axis=0)
 
 
 def whole_kernel(cfg, *refs):
-    (row_count, col_count, inner, cuts, factor, fused) = cfg
+    (row_count, col_count, inner, turns, parts, factor, fused) = cfg
     refs = list(refs)
     take = lambda n: [refs.pop(0) for _ in range(n)]
-    occ_ref, vir_ref, occ_decay, vir_decay = take(4)
+    occ_ref, vir_ref, decays = take(3)
     if fused:
         (table_hbm,) = take(1)
         parts_out = take(2 * PIECES)
-        tail_x, tail_cos, tail_sin, tail_line, tail_swap = take(5)
+        tail_x, tail_cos, tail_sin, tail_line = take(4)
     else:
         (x_ref,) = take(1)
     planes = take(2)
@@ -177,10 +193,10 @@
     lefts = take(2)
     mixed, polar, swap = take(3)
     if fused:
-        x_ref, piece_swap, line_ref, cos_ref, sin_ref, lines_buf, acc_re, acc_im = take(8)
+        x_ref, line_ref, plane_ref, lines_buf, acc_ref = take(5)
         table_sem, out_sem, tail_sem = take(3)
     (wave_send, wave_recv, col_send, col_recv, line_send, line_recv, share_send, share_recv) = take(8)
-    (give_send, give_recv, pass_send, pass_recv, local) = take(5)
+    (give_send, give_recv, pass_send, pass_recv, local, col_local, keep_sem) = take(7)
 
     row, col = lax.axis_index("row"), lax.axis_index("col")
     outer = row_count // inner
@@ -197,28 +213,34 @@
     barrier, arrivals = enter(row_count, col_count, inner, row, col)
 
     own = []
-    for i in range(2):
-        lanes = pl.ds(pl.multiple_of(row * points, LANES), points)
-        own.append(pltpu.make_async_copy(waves[i].at[:, lanes], planes[i].at[row], local.at[i]))
+    span = points // turns
+
+    def share_of(to, turn):
+        return (lax.div(to, turns) * turns + turn) * points + lax.rem(to, turns) * span
+
+    for turn in range(turns):
+        for i in range(2):
+            lanes = pl.ds(pl.multiple_of(share_of(row, turn), LANES), span)
+            place = planes[i].at[row, :, pl.ds(turn * span, span)]
+            own.append(pltpu.make_async_copy(waves[i].at[:, lanes], place, local.at[turn, i]))
     if fused:
         width = line_ref.shape[0]
         lines = pl.ds(pl.multiple_of(2 * NAB + col * width, width), width)
         own.append(pltpu.make_async_copy(table_hbm.at[lines, pl.ds(0, width)], line_ref, table_sem.at[0]))
-        own.append(pltpu.make_async_copy(table_hbm.at[pl.ds(0, NAB)], cos_ref, table_sem.at[1]))
-        own.append(pltpu.make_async_copy(table_hbm.at[pl.ds(NAB, NAB)], sin_ref, table_sem.at[2]))
+        own.append(pltpu.make_async_copy(table_hbm.at[pl.ds(0, 2 * NAB)], plane_ref, table_sem.at[1]))
     for copy in own:
         copy.start()
     pl.semaphore_wait(barrier, arrivals)
 
     def start_waves(part, ks):
-        first, last = cuts[part], cuts[part + 1]
+        turn, first, last = parts[part]
         for k in ks:
             to = peer(k)
-            lanes = pl.ds(pl.multiple_of(to * points + first, LANES), last - first)
+            lanes = pl.ds(pl.multiple_of(share_of(to, turn) + first, LANES), last - first)
             for i in range(2):
                 copy = send(
                     waves[i].at[:, lanes],
-                    planes[i].at[row, :, pl.ds(first, last - first)],
+                    planes[i].at[row, :, pl.ds(turn * span + first, last - first)],
                     wave_send.at[i],
                     wave_recv.at[i, part],
                     (to, col),
@@ -226,11 +248,11 @@
                 copy.start()
 
     def wait_waves(part):
-        lanes = pl.ds(cuts[part], cuts[part + 1] - cuts[part])
+        turn, first, last = parts[part]
+        lanes = pl.ds(turn * span + first, last - first)
         for i in range(2):
             drain(planes[i].at[pl.ds(0, row_count - 1), :, lanes], wave_recv.at[i, part])
 
-    parts = len(cuts) - 1
     near = row_count // 2
 
     def slab_share(c):
@@ -251,24 +273,34 @@
             for c in range(1, col_count):
                 over_col(i, c).start()
             pltpu.make_async_copy(
-                waves[i].at[:, slab_share(0)], raws[i].at[mine, seat, :, slab_share(0)], local.at[2 + i]
+                waves[i].at[:, slab_share(0)], raws[i].at[mine, seat, :, slab_share(0)], col_local.at[i]
             ).start()
 
     far = range(near, row_count)
-    queue = [k for s in range(inner) for k in far if k % inner == s]
-    queue += [k for k in range(inner, near)] + [k for k in range(1, inner)]
-
-    def advance(count):
-        start_waves(0, queue[:count])
-        del queue[:count]
-
-    advance(1)
+    seats = [[k for k in far if k % inner == s] for s in range(inner)]
+    count = len(parts)
+    middle = inner // 2
+    near_all = list(range(inner, near)) + list(range(1, inner))
+    far_straight = [k for ks in seats[:middle] for k in ks]
+    far_turned = [k for ks in seats[middle:] for k in ks]
+    straight = [(part, k) for part in range(count) for k in far_straight]
+    turned = [(part, k) for part in range(count) for k in far_turned]
+
+    def advance(some):
+        for part, k in some:
+            start_waves(part, [k])
+
+    def ahead(count):
+        advance(straight[:count])
+        del straight[:count]
+
+    ahead(1)
 
     @pl.when(col == 0)
     def _():
         for i in range(2):
             pltpu.make_async_copy(
-                waves[i].at[:, slab_share(0)], raws[i].at[mine, seat, :, slab_share(0)], local.at[2 + i]
+                waves[i].at[:, slab_share(0)], raws[i].at[mine, seat, :, slab_share(0)], col_local.at[i]
             ).wait()
 
     if col_count > 1:
@@ -301,7 +333,7 @@
         )
         number += len(held)
         held = held + [mask + bit for mask in held]
-        advance(1)
+        ahead(AHEAD[0] if bit * 2 >= outer else AHEAD[1])
         for copy in started:
             copy.wait_recv()
     started = []
@@ -313,7 +345,7 @@
     for copy in started:
         copy.start()
     sent.extend(started)
-    advance(1)
+    ahead(AHEAD[2])
     for copy in started:
         copy.wait_recv()
     held = [0]
@@ -328,37 +360,31 @@
         )
         number += len(held)
         held = held + [mask + bit for mask in held]
-        advance(2)
+        if bit * 2 >= inner:
+            advance(turned[: len(far_turned) // 2])
+        else:
+            advance(turned[len(far_turned) // 2 : len(far_turned)])
+            advance((0, k) for k in near_all)
+            ahead(len(straight))
         for copy in started:
             copy.wait_recv()
-    advance(len(queue))
-    order = [k for k in far] + [k for k in range(inner, near)] + [k for k in range(1, inner)]
-    for part in range(1, parts):
-        start_waves(part, order)
-
-    per_point = points // NC
-    fill(swap, lambda p, n: n == (p & (NC - 1)) * per_point + lax.div(p, NC), min(LANES, points))
+    advance(turned[len(far_turned) :])
+    advance((part, k) for part in range(1, count) for k in near_all)
+
+    per_point = span // NC
+    fill(swap, lambda p, n: n == (p & (NC - 1)) * per_point + lax.div(p, NC), min(LANES, span))
     if fused:
-        per = LANES // NB
-        inside = per * NB
-
-        def piece(p, n):
-            k, j, w = lax.div(p, inside), lax.div(p & (inside - 1), NB), p & (NB - 1)
-            return n == j * inside + k * NB + w
-
-        fill(piece_swap, piece, LANES)
-        acc_re[...] = jnp.zeros_like(acc_re)
-        acc_im[...] = jnp.zeros_like(acc_im)
-
-    for i, decay in enumerate((occ_decay, vir_decay)):
+        acc_ref[...] = jnp.zeros_like(acc_ref)
+
+    for i, start in enumerate((0, lefts[0].shape[1])):
         raw, left = raws[i], lefts[i]
         bands = raw.shape[2]
         join = max(1, LANES // (inner * bands))
         width = join * inner * bands
 
-        def scale(m, carry, raw=raw, left=left, decay=decay, width=width, join=join):
+        def scale(m, carry, raw=raw, left=left, start=start, width=width, join=join):
             lanes = pl.ds(pl.multiple_of(m * width, width), width)
-            factors = decay[:, lanes]
+            factors = decays[:, pl.ds(pl.multiple_of(start + m * width, LANES), width)]
             for t in range(window // LANES):
                 piece = raw[pl.ds(m * join, join), :, :, pl.ds(t * LANES, LANES)]
                 turned = piece.reshape(width, LANES).astype(jnp.float32).T * factors
@@ -371,18 +397,18 @@
 
         lax.fori_loop(0, outer // join, scale, 0)
 
-    def product(h, first, width):
+    def product(h, turn, first, width):
         rows = pl.ds(h * block_rows, block_rows)
-        lanes = pl.ds(first, width)
+        lanes = pl.ds(turn * span + first, width)
         green = []
         for i in range(2):
             wave = planes[i][:, :, lanes]
             wave = wave.reshape(wave.shape[0] * wave.shape[1], width)
             green.append(dot(lefts[i][rows, :], wave))
         value = (green[0] * green[1] * factor).astype(jnp.bfloat16)
-        return dot(value, swap[lanes, :])
-
-    for copy in own[:2]:
+        return dot(value, swap[pl.ds(first, width), :])
+
+    for copy in own[: 2 * turns]:
         copy.wait()
     ordered = [k for s in range(inner) for k in far if k % inner == s]
     quarter = len(ordered) // FARS
@@ -402,9 +428,12 @@
     def to_cols(h, ks):
         for k in ks:
             for d in range(1, col_count):
+                slot = x_ref.at[h, col, row]
+                if fused and h == turns * HALVES - 1:
+                    slot = tail_x.at[d - 1, row]
                 send(
                     polar.at[h, peer(k)],
-                    x_ref.at[h, col, row],
+                    slot,
                     pass_send.at[h],
                     pass_recv.at[h, d - 1, 0],
                     (peer(k), lax.rem(col + d, col_count)),
@@ -417,8 +446,8 @@
             arrived = x_ref.at[h, col, peer(k)]
             for d in range(1, col_count):
                 slot = arrived
-                if fused and h == HALVES - 1:
-                    slot = tail_x.at[d - 1, lax.rem(peer(k), near)]
+                if fused and h == turns * HALVES - 1:
+                    slot = tail_x.at[d - 1, peer(k)]
                 to = (row, lax.rem(col + d, col_count))
                 send(arrived, slot, pass_send.at[h], pass_recv.at[h, d - 1, 1], to).start()
 
@@ -432,7 +461,7 @@
             drain(x_ref.at[h, col, pl.ds(0, count)], pass_recv.at[h, d - 1, which])
 
     def give(h):
-        copy = pltpu.make_async_copy(polar.at[h, row], x_ref.at[h, col, row], local.at[2 + h])
+        copy = pltpu.make_async_copy(polar.at[h, row], x_ref.at[h, col, row], keep_sem.at[h])
         copy.start()
         keep.append(copy)
         to_cols(h, range(min(2, inner)))
@@ -442,63 +471,59 @@
         to_row(h, range(1, inner), 0)
         to_cols(h, range(min(2, inner), near))
 
-    for part in range(parts):
+    def form(part):
         wait_waves(part)
-        first, last = cuts[part], cuts[part + 1]
+        turn, first, last = parts[part]
         tile = min(last - first, 2 * LANES)
         for h in range(HALVES):
-            moved = mixed[h] if part else None
+            moved = mixed[h] if first else None
             for start in range(first, last, tile):
-                term = product(h, start, tile)
+                term = product(h, turn, start, tile)
                 moved = term if moved is None else moved + term
-            if part < parts - 1:
+            if last < span:
                 mixed[h] = moved
             else:
-                polar[h] = moved.astype(jnp.bfloat16).reshape(row_count, HALF_ROWS, points)
-                give(h)
+                g = turn * HALVES + h
+                polar[g] = moved.astype(jnp.bfloat16).reshape(row_count, HALF_ROWS, span)
+                give(g)
 
     if fused:
-        for copy in own[2:]:
+        for copy in own[2 * turns :]:
             copy.wait()
-        per = LANES // NB
-        side = lax.div(row, near)
-        other = 1 - side
-
-        wide = near * NB
+        wide = 2 * row_count * per_point
+        middle = wide // 2
         tails = [
             pltpu.make_async_copy(line_ref, tail_line, tail_sem.at[0]),
-            pltpu.make_async_copy(piece_swap, tail_swap, tail_sem.at[1]),
         ]
         for d in range(1, col_count):
             c = lax.rem(col + col_count - d, col_count)
-            depth = pl.ds(pl.multiple_of((c * 2 + other) * wide, wide), wide)
-            tails.append(pltpu.make_async_copy(cos_ref.at[depth], tail_cos.at[d - 1], tail_sem.at[2 * d]))
-            tails.append(pltpu.make_async_copy(sin_ref.at[depth], tail_sin.at[d - 1], tail_sem.at[2 * d + 1]))
+            depth = pl.multiple_of((c * turns + turns - 1) * wide, wide)
+            for n, tail in enumerate((tail_cos, tail_sin)):
+                part = plane_ref.at[pl.ds(depth + n * middle, middle)]
+                tails.append(pltpu.make_async_copy(part, tail.at[d - 1], tail_sem.at[2 * d + n]))
         for copy in tails:
             copy.start()
 
-        def transform(h, c, z):
-            blocks = [x_ref.at[h, c, z * near + a] for a in range(near)]
-            re, im = spread(blocks, piece_swap, lines_buf, line_ref)
-            depth = pl.ds(pl.multiple_of((c * 2 + z) * wide, wide), wide)
-            cosine, sine = cos_ref[depth, :], sin_ref[depth, :]
-            acc_re[h] += dot(re, cosine) + dot(im, sine)
-            acc_im[h] += dot(im, cosine) - dot(re, sine)
+        def transform(g, c):
+            turn, h = divmod(g, HALVES)
+            blocks = [x_ref.at[g, c, q] for q in range(row_count)]
+            depth = pl.ds(pl.multiple_of((c * turns + turn) * wide, wide), wide)
+            acc_ref[h] += dot(spread(blocks, lines_buf, line_ref), plane_ref[depth, :])
 
         def put_out(h):
             per_half = PIECES // HALVES
-            height = acc_re.shape[1] // per_half
-            for i, acc in enumerate((acc_re, acc_im)):
+            height = acc_ref.shape[1] // (2 * per_half)
+            for i in range(2):
                 for n in range(per_half):
-                    p = i * PIECES + h * per_half + n
                     pltpu.make_async_copy(
-                        acc.at[h, pl.ds(n * height, height)], parts_out[p], out_sem.at[h]
+                        acc_ref.at[h, pl.ds((i * per_half + n) * height, height)],
+                        parts_out[i * PIECES + h * per_half + n],
+                        out_sem.at[h],
                     ).start()
 
     else:
-        side = other = 0
-
-        def transform(h, c, z):
+
+        def transform(g, c):
             return
 
         def put_out(h):
@@ -506,43 +531,49 @@
 
         tails = []
     others = [lax.rem(col + d, col_count) for d in range(1, col_count)]
-    forward(0, 0)
-    forward(0, 1)
-    wait_near(0)
-    transform(0, col, side)
-    forward(0, 2)
-    forward(0, 3)
-    wait_pass(0, 0)
-    for c in others:
-        transform(0, c, side)
-    transform(0, col, other)
-    forward(1, 0)
-    forward(1, 1)
-    wait_near(1)
-    transform(1, col, side)
-    forward(1, 2)
-    wait_pass(0, 1)
-    for c in others:
-        transform(0, c, other)
-    put_out(0)
-    wait_pass(1, 0)
-    for c in others:
-        transform(1, c, side)
-    forward(1, 3)
-    transform(1, col, other)
-    put_out(1)
-    wait_pass(1, 1)
+
+    def wait_passes(g):
+        wait_pass(g, 0)
+        wait_pass(g, 1)
+
+    for part in range(len(parts)):
+        form(part)
+    last = turns * HALVES - 1
+    pending = []
+
+    def settle():
+        g = pending.pop(0)
+        wait_passes(g)
+        for c in others:
+            transform(g, c)
+        if g + HALVES > last:
+            put_out(g % HALVES)
+
+    for g in range(last + 1):
+        for group in range(FARS // 2):
+            forward(g, group)
+        if len(pending) > 1:
+            settle()
+        for group in range(FARS // 2, FARS):
+            forward(g, group)
+        wait_near(g)
+        transform(g, col)
+        pending.append(g)
+    put_out(last % HALVES)
+    while len(pending) > 1:
+        settle()
+    wait_passes(last)
     for copy in tails:
         copy.wait()
     if fused:
         for h in range(HALVES):
-            drain(acc_re, out_sem.at[h])
+            drain(acc_ref.at[h], out_sem.at[h])
 
     for i in range(2):
         drain(planes[i].at[pl.ds(0, row_count - 1)], wave_send.at[i])
     for copy in sent:
         copy.wait_send()
-    for h in range(HALVES):
+    for h in range(turns * HALVES):
         drain(x_ref.at[h, col, pl.ds(0, row_count - 1)], give_send.at[h])
         for d in range(1, col_count):
             drain(x_ref.at[h, col], pass_send.at[h])
@@ -554,66 +585,66 @@
                 over_col(i, c).wait_send()
 
     if not fused:
-        for copy in own[2:]:
+        for copy in own[2 * turns :]:
             copy.wait()
 
 
-def whole(row_count, col_count, occ, vir, occ_decay, vir_decay, window, factor):
+def whole(row_count, col_count, occ, vir, decays, window, factor):
     inner = group_size(row_count)
     outer = row_count // inner
     points = occ.shape[1] // row_count
     fused = points == NB * NC and row_count * col_count == NA and (row_count // 2) % (LANES // NB) == 0
-    quarter = points // 4
-    cuts = (0, points - quarter, points) if quarter % LANES == 0 else (0, points)
-    parts = len(cuts) - 1
+    fused = fused and row_count % 2 == 0
+    turns = 2 if fused else 1
+    span = points // turns
+    parts = tuple((turn, 0, span) for turn in range(turns))
     bands = (occ.shape[0], vir.shape[0])
     block_rows = row_count * HALF_ROWS
     bf16, f32 = jnp.bfloat16, jnp.float32
     dma = pltpu.SemaphoreType.DMA
     vmem = pl.BlockSpec(memory_space=pltpu.VMEM)
     hbm = pl.BlockSpec(memory_space=pltpu.HBM)
-    x_shape = (HALVES, col_count, row_count, HALF_ROWS, points)
-    operands = [occ, vir, occ_decay, vir_decay]
-    in_specs = [hbm, hbm, vmem, vmem]
+    x_shape = (turns * HALVES, col_count, row_count, HALF_ROWS, span)
+    operands = [occ, vir, decays]
+    in_specs = [hbm, hbm, vmem]
     scratch = [pltpu.VMEM((row_count, b, points), bf16) for b in bands]
     scratch += [pltpu.VMEM((outer, inner, b, window), bf16) for b in bands]
     scratch += [pltpu.VMEM((window, row_count * b), bf16) for b in bands]
     scratch += [
-        pltpu.VMEM((HALVES, block_rows, points), f32),
-        pltpu.VMEM((HALVES, row_count, HALF_ROWS, points), bf16),
-        pltpu.VMEM((points, points), bf16),
+        pltpu.VMEM((HALVES, block_rows, span), f32),
+        pltpu.VMEM((turns * HALVES, row_count, HALF_ROWS, span), bf16),
+        pltpu.VMEM((span, span), bf16),
     ]
     if fused:
-        cosine, sine = plane_tables()
+        cosine, sine = plane_tables(turns, row_count)
+        depth = row_count * (span // NC)
+        both = jnp.stack([cosine.reshape(-1, depth, NAB), sine.reshape(-1, depth, NAB)], axis=1)
         line = line_tables(col_count)
         flat = jnp.pad(line.reshape(-1, line.shape[2]), ((0, 0), (0, NAB - line.shape[2])))
-        operands += [jnp.concatenate([cosine, sine, flat])]
+        operands += [jnp.concatenate([both.reshape(-1, NAB), flat])]
         in_specs += [hbm]
-        wide = (LANES // NB) * LANES
         scratch += [
             pltpu.VMEM(x_shape, bf16),
-            pltpu.VMEM((wide, wide), bf16),
             pltpu.VMEM(line.shape[1:], bf16),
-            pltpu.VMEM(cosine.shape, bf16),
-            pltpu.VMEM(sine.shape, bf16),
-            pltpu.VMEM((NC * R_BLOCK, (row_count // 2) * NB), bf16),
+            pltpu.VMEM((2 * NAB, NAB), bf16),
+            pltpu.VMEM((NC * R_BLOCK, row_count * (span // NC)), bf16),
         ]
-        scratch += [pltpu.VMEM((HALVES, line.shape[1] // 2, NAB), f32)] * 2
-        scratch += [dma((3,)), dma((HALVES,)), dma((2 * col_count,))]
+        scratch += [pltpu.VMEM((HALVES, line.shape[1], NAB), f32)]
+        scratch += [dma((2,)), dma((HALVES,)), dma((2 * col_count,))]
         out_shape = [jax.ShapeDtypeStruct((HALVES * line.shape[1] // 2 // PIECES, NAB), f32)] * (2 * PIECES)
         late = col_count - 1
-        near = row_count // 2
-        tails = [(late, near, HALF_ROWS, points)] + [(late, near * NB, NAB)] * 2 + [line.shape[1:], (wide, wide)]
+        tails = [(late, row_count, HALF_ROWS, span)] + [(late, depth, NAB)] * 2 + [line.shape[1:]]
         out_shape += [jax.ShapeDtypeStruct(shape, bf16) for shape in tails]
     else:
         out_shape = [jax.ShapeDtypeStruct(x_shape, bf16)]
     places = max(1, col_count - 1)
     steps = outer - 1 + inner - 1
-    scratch += [dma((2,)), dma((2, parts)), dma((2, places)), dma((2,))]
+    scratch += [dma((2,)), dma((2, len(parts))), dma((2, places)), dma((2,))]
     scratch += [dma((2, steps))] * 2 + [dma((2, places))] * 2
-    scratch += [dma((HALVES,)), dma((HALVES, 1 + FARS)), dma((HALVES,)), dma((HALVES, places, 2))]
-    scratch += [dma((4,))]
-    cfg = (row_count, col_count, inner, cuts, factor, fused)
+    gives = turns * HALVES
+    scratch += [dma((gives,)), dma((gives, 1 + FARS)), dma((gives,)), dma((gives, places, 2))]
+    scratch += [dma((turns, 2)), dma((2,)), dma((gives,))]
+    cfg = (row_count, col_count, inner, turns, parts, factor, fused)
     result = pl.pallas_call(
         functools.partial(whole_kernel, cfg),
         out_shape=out_shape,
@@ -629,7 +660,8 @@
 
 def last_kernel(*refs):
     parts = refs[: 2 * PIECES]
-    tail_x, tail_cos, tail_sin, tail_line, tail_swap, re_out, im_out, lines_buf, *acc, sems = refs[2 * PIECES :]
+    tail_x, tail_cos, tail_sin, tail_line = refs[2 * PIECES : 2 * PIECES + 4]
+    re_out, im_out, lines_buf, *acc, sems = refs[2 * PIECES + 4 :]
     outs = (re_out, im_out)
     half = PIECES // HALVES
     rows = parts[0].shape[0]
@@ -646,18 +678,15 @@
     late = []
     for d in range(tail_x.shape[0]):
         blocks = [tail_x.at[d, a] for a in range(tail_x.shape[1])]
-        re, im = spread(blocks, tail_swap, lines_buf, tail_line)
-        late.append((re, im, tail_cos[d], tail_sin[d]))
+        late.append((spread(blocks, lines_buf, tail_line), tail_cos[d], tail_sin[d]))
     for n in range(half):
         p = half + n
-        at = slice(n * rows, (n + 1) * rows)
         for i in range(2):
             total = parts[i * PIECES + p][...]
-            for re, im, cosine, sine in late:
-                if i == 0:
-                    total = total + (dot(re[at], cosine) + dot(im[at], sine))
-                else:
-                    total = total + (dot(im[at], cosine) - dot(re[at], sine))
+            for both, cosine, sine in late:
+                some = both[(i * half + n) * rows : (i * half + n + 1) * rows]
+                middle = some.shape[1] // 2
+                total = total + dot(some[:, :middle], cosine) + dot(some[:, middle:], sine)
             acc[i][pl.ds(n * rows, rows), :] = total
             put(i, p, acc[i].at[pl.ds(n * rows, rows)])
     for copy in copies:
@@ -675,7 +704,7 @@
         in_specs=[vmem] * len(operands),
         out_specs=[pl.BlockSpec(memory_space=pltpu.HBM)] * 2,
         scratch_shapes=[
-            pltpu.VMEM((NC * R_BLOCK, tail_x.shape[1] * NB), jnp.bfloat16),
+            pltpu.VMEM((NC * R_BLOCK, operands[2 * PIECES + 1].shape[1]), jnp.bfloat16),
             acc,
             acc,
             pltpu.SemaphoreType.DMA((2, PIECES)),
@@ -696,8 +725,7 @@
         col_count,
         occupied_waves,
         virtual_waves,
-        occupied_decay.reshape(1, nocc),
-        virtual_decay.reshape(1, nvir),
+        jnp.concatenate([occupied_decay, virtual_decay]).reshape(1, nocc + nvir),
         window,
         factor,
     )

time: 115 us -> 109 us (0.948)
  Pallas kernels: 112 us -> 107 us
  local copies, waits for them, and re-layouts: 1.36 us -> 0.01 us
    pallas_call x1, Pallas kernels: 109 us -> 105 us  [whole(): pl.pallas_call(functools.partial(whole_kernel, cfg), out_shape=out_shape,...]
    unnamed x4 -> x0, local copies, waits for them, and re-layouts: 1.36 us -> none
where the time goes in v3:
time: 109 us
  Pallas kernels  107 us (98%)
    pallas_call x1, Pallas kernels, whole(): pl.pallas_call(functools.partial(whole_kernel, cfg), out_shape=out_shape,...  105 us
    pallas_call x1, Pallas kernels, last(): pl.pallas_call(last_kernel, out_shape=[jax.ShapeDtypeStruct((rows * PIECE...  2.43 us

profile of v3, /device:TPU:0, one launch (start us, length us, event | category | flops | bytes accessed | tf_op | source)
XLA Modules:
  0.0 108.6 jit_solution(15045312280074887262)
XLA Ops:
  0.6 0.7 pad_maximum_fusion
  1.3 104.8 %shard_map.86 = (f32[128,1024]{1,0:T(8,128)S(1)}, f32[128,1024]{1,0:T(8,128)S(1)}, f32[128,1024]{1,0:T(8,128)S(1)}, f32[128,1024]{1,0:T(8,128)S(1)}, f32[128,102...) custom-call(bf16[64,16384]{1,0:T(8,128)(2,1)} %refs_0_.1, ...), custom_call_target="tpu_custom_call" | custom-call | tf_op jit(solution)/shard_map/pallas_call | solution.py:648
  106.2 2.4 %shard_map.87 = (f32[512,1024]{1,0:T(8,128)}, f32[512,1024]{1,0:T(8,128)}) custom-call(f32[128,1024]{1,0:T(8,128)S(1)} %get-tuple-element.16.refs_0_, f32[128,1024]{1,0:T(8,128)S(1)} %get-tuple-element.17.refs_1_, f32[128,1024]{1,0:T(8,128)S(1)} %get-tuple-element.18.refs_2_, f32[128,1024]{1,0:T(8,128)S(1)} %get-tuple-element.19.refs_3_, ...), custom_call_target="tpu_custom_call" | custom-call | tf_op jit(solution)/shard_map/pallas_call | solution.py:701
  (1 shorter events, 0.0 us)

commit v4 on v3

--- a/solution.py
+++ b/solution.py
@@ -27,13 +27,19 @@
     return jnp.asarray(table.astype(np.float32)).astype(jnp.bfloat16)
 
 
-def plane_tables(turns, group):
+def plane_tables():
     index = np.arange(NAB)
     a, b = index // NB, index % NB
     phase = a[:, None] * a[None, :] * NB + b[:, None] * b[None, :] * NA
-    rows = index.reshape(-1, group // turns, turns, NB).transpose(0, 2, 1, 3).reshape(-1)
-    cosine, sine = trig(phase[rows], NA * NB)
+    cosine, sine = trig(phase, NA * NB)
     return bf16_table(cosine), bf16_table(sine)
+
+
+def angle_tables():
+    index = np.arange(NAB)
+    first = trig(np.arange(NA)[:, None] * (index // NB)[None, :], NA)
+    second = trig(np.arange(NB)[:, None] * (index % NB)[None, :], NB)
+    return jnp.asarray(np.concatenate(first + second).astype(np.float32))
 
 
 def line_tables(col_count):
@@ -63,7 +69,7 @@
 
 def spectrum(x, line_table):
     r_count = x.shape[1]
-    cosine, sine = plane_tables(1, NA)
+    cosine, sine = plane_tables()
     out_rows = line_table.shape[1] // 2
     steps = r_count // R_BLOCK
     whole = lambda table: pl.BlockSpec(table.shape, lambda i: (0,) * table.ndim)
@@ -183,7 +189,7 @@
     take = lambda n: [refs.pop(0) for _ in range(n)]
     occ_ref, vir_ref, decays = take(3)
     if fused:
-        (table_hbm,) = take(1)
+        line_hbm, angle_hbm = take(2)
         parts_out = take(2 * PIECES)
         tail_x, tail_cos, tail_sin, tail_line = take(4)
     else:
@@ -193,7 +199,7 @@
     lefts = take(2)
     mixed, polar, swap = take(3)
     if fused:
-        x_ref, line_ref, plane_ref, lines_buf, acc_ref = take(5)
+        x_ref, line_ref, angle_ref, plane_ref, lines_buf, acc_ref = take(6)
         table_sem, out_sem, tail_sem = take(3)
     (wave_send, wave_recv, col_send, col_recv, line_send, line_recv, share_send, share_recv) = take(8)
     (give_send, give_recv, pass_send, pass_recv, local, col_local, keep_sem) = take(7)
@@ -224,10 +230,8 @@
             place = planes[i].at[row, :, pl.ds(turn * span, span)]
             own.append(pltpu.make_async_copy(waves[i].at[:, lanes], place, local.at[turn, i]))
     if fused:
-        width = line_ref.shape[0]
-        lines = pl.ds(pl.multiple_of(2 * NAB + col * width, width), width)
-        own.append(pltpu.make_async_copy(table_hbm.at[lines, pl.ds(0, width)], line_ref, table_sem.at[0]))
-        own.append(pltpu.make_async_copy(table_hbm.at[pl.ds(0, 2 * NAB)], plane_ref, table_sem.at[1]))
+        own.append(pltpu.make_async_copy(line_hbm.at[col], line_ref, table_sem.at[0]))
+        own.append(pltpu.make_async_copy(angle_hbm, angle_ref, table_sem.at[1]))
     for copy in own:
         copy.start()
     pl.semaphore_wait(barrier, arrivals)
@@ -375,6 +379,22 @@
     fill(swap, lambda p, n: n == (p & (NC - 1)) * per_point + lax.div(p, NC), min(LANES, span))
     if fused:
         acc_ref[...] = jnp.zeros_like(acc_ref)
+        for copy in own[2 * turns :]:
+            copy.wait()
+        depth = row_count * per_point
+
+        def fill_planes(a, carry):
+            within = lax.rem(a, row_count)
+            turn = lax.div(a, row_count) * turns + lax.rem(within, turns)
+            at = turn * 2 * depth + lax.div(within, turns) * NB
+            cos_a, sin_a = angle_ref[pl.ds(a, 1), :], angle_ref[pl.ds(NA + a, 1), :]
+            cos_b, sin_b = angle_ref[pl.ds(2 * NA, NB), :], angle_ref[pl.ds(2 * NA + NB, NB), :]
+            cosine, sine = cos_a * cos_b - sin_a * sin_b, sin_a * cos_b + cos_a * sin_b
+            plane_ref[pl.ds(pl.multiple_of(at, NB), NB), :] = cosine.astype(jnp.bfloat16)
+            plane_ref[pl.ds(pl.multiple_of(at + depth, NB), NB), :] = sine.astype(jnp.bfloat16)
+            return carry
+
+        lax.fori_loop(0, NA, fill_planes, 0)
 
     for i, start in enumerate((0, lefts[0].shape[1])):
         raw, left = raws[i], lefts[i]
@@ -488,8 +508,6 @@
                 give(g)
 
     if fused:
-        for copy in own[2 * turns :]:
-            copy.wait()
         wide = 2 * row_count * per_point
         middle = wide // 2
         tails = [
@@ -616,16 +634,14 @@
         pltpu.VMEM((span, span), bf16),
     ]
     if fused:
-        cosine, sine = plane_tables(turns, row_count)
+        line, angles = line_tables(col_count), angle_tables()
         depth = row_count * (span // NC)
-        both = jnp.stack([cosine.reshape(-1, depth, NAB), sine.reshape(-1, depth, NAB)], axis=1)
-        line = line_tables(col_count)
-        flat = jnp.pad(line.reshape(-1, line.shape[2]), ((0, 0), (0, NAB - line.shape[2])))
-        operands += [jnp.concatenate([both.reshape(-1, NAB), flat])]
-        in_specs += [hbm]
+        operands += [line, angles]
+        in_specs += [hbm] * 2
         scratch += [
             pltpu.VMEM(x_shape, bf16),
             pltpu.VMEM(line.shape[1:], bf16),
+            pltpu.VMEM(angles.shape, f32),
             pltpu.VMEM((2 * NAB, NAB), bf16),
             pltpu.VMEM((NC * R_BLOCK, row_count * (span // NC)), bf16),
         ]

time: 109 us -> 109 us (level)
  no operation moved by 1% of the time
where the time goes in v4:
time: 109 us
  Pallas kernels  107 us (98%)
    pallas_call x1, Pallas kernels, whole(): pl.pallas_call(functools.partial(whole_kernel, cfg), out_shape=out_shape,...  105 us
    pallas_call x1, Pallas kernels, last(): pl.pallas_call(last_kernel, out_shape=[jax.ShapeDtypeStruct((rows * PIECE...  2.43 us

profile of v4, /device:TPU:0, one launch (start us, length us, event | category | flops | bytes accessed | tf_op | source)
XLA Modules:
  0.0 108.6 jit_solution(8125742479583201107)
XLA Ops:
  0.6 0.7 pad_maximum_fusion
  1.3 104.8 %shard_map.77 = (f32[128,1024]{1,0:T(8,128)S(1)}, f32[128,1024]{1,0:T(8,128)S(1)}, f32[128,1024]{1,0:T(8,128)S(1)}, f32[128,1024]{1,0:T(8,128)S(1)}, f32[128,102...) custom-call(bf16[64,16384]{1,0:T(8,128)(2,1)} %refs_0_.1, ...), custom_call_target="tpu_custom_call" | custom-call | tf_op jit(solution)/shard_map/pallas_call | solution.py:664
  106.2 2.4 %shard_map.78 = (f32[512,1024]{1,0:T(8,128)}, f32[512,1024]{1,0:T(8,128)}) custom-call(f32[128,1024]{1,0:T(8,128)S(1)} %get-tuple-element.16.refs_0_, f32[128,1024]{1,0:T(8,128)S(1)} %get-tuple-element.17.refs_1_, f32[128,1024]{1,0:T(8,128)S(1)} %get-tuple-element.18.refs_2_, f32[128,1024]{1,0:T(8,128)S(1)} %get-tuple-element.19.refs_3_, ...), custom_call_target="tpu_custom_call" | custom-call | tf_op jit(solution)/shard_map/pallas_call | solution.py:717
  (1 shorter events, 0.0 us)

commit v5 on v4

--- a/solution.py
+++ b/solution.py
@@ -440,7 +440,7 @@
             send(
                 polar.at[h, peer(k)],
                 x_ref.at[h, col, row],
-                give_send.at[h],
+                give_send.at[0],
                 give_recv.at[h, group],
                 (peer(k), col),
             ).start()
@@ -454,7 +454,7 @@
                 send(
                     polar.at[h, peer(k)],
                     slot,
-                    pass_send.at[h],
+                    pass_send.at[0],
                     pass_recv.at[h, d - 1, 0],
                     (peer(k), lax.rem(col + d, col_count)),
                 ).start()
@@ -469,7 +469,7 @@
                 if fused and h == turns * HALVES - 1:
                     slot = tail_x.at[d - 1, peer(k)]
                 to = (row, lax.rem(col + d, col_count))
-                send(arrived, slot, pass_send.at[h], pass_recv.at[h, d - 1, 1], to).start()
+                send(arrived, slot, pass_send.at[0], pass_recv.at[h, d - 1, 1], to).start()
 
     def wait_near(h):
         drain(x_ref.at[h, col, pl.ds(0, near - 1)], give_recv.at[h, 0])
@@ -591,10 +591,9 @@
         drain(planes[i].at[pl.ds(0, row_count - 1)], wave_send.at[i])
     for copy in sent:
         copy.wait_send()
-    for h in range(turns * HALVES):
-        drain(x_ref.at[h, col, pl.ds(0, row_count - 1)], give_send.at[h])
-        for d in range(1, col_count):
-            drain(x_ref.at[h, col], pass_send.at[h])
+    drain(x_ref.at[:, 0, pl.ds(0, row_count - 1)], give_send.at[0])
+    for d in range(1, col_count):
+        drain(x_ref.at[:, 0], pass_send.at[0])
 
     @pl.when(col == 0)
     def _():
@@ -658,7 +657,7 @@
     scratch += [dma((2,)), dma((2, len(parts))), dma((2, places)), dma((2,))]
     scratch += [dma((2, steps))] * 2 + [dma((2, places))] * 2
     gives = turns * HALVES
-    scratch += [dma((gives,)), dma((gives, 1 + FARS)), dma((gives,)), dma((gives, places, 2))]
+    scratch += [dma((1,)), dma((gives, 1 + FARS)), dma((1,)), dma((gives, places, 2))]
     scratch += [dma((turns, 2)), dma((2,)), dma((gives,))]
     cfg = (row_count, col_count, inner, turns, parts, factor, fused)
     result = pl.pallas_call(

time: 109 us -> 109 us (level)
  no operation moved by 1% of the time
where the time goes in v5:
time: 109 us
  Pallas kernels  107 us (98%)
    pallas_call x1, Pallas kernels, whole(): pl.pallas_call(functools.partial(whole_kernel, cfg), out_shape=out_shape,...  105 us
    pallas_call x1, Pallas kernels, last(): pl.pallas_call(last_kernel, out_shape=[jax.ShapeDtypeStruct((rows * PIECE...  2.43 us

profile of v5, /device:TPU:0, one launch (start us, length us, event | category | flops | bytes accessed | tf_op | source)
XLA Modules:
  0.0 108.5 jit_solution(12021505948062785869)
XLA Ops:
  0.6 0.7 pad_maximum_fusion
  1.3 104.7 %shard_map.77 = (f32[128,1024]{1,0:T(8,128)S(1)}, f32[128,1024]{1,0:T(8,128)S(1)}, f32[128,1024]{1,0:T(8,128)S(1)}, f32[128,1024]{1,0:T(8,128)S(1)}, f32[128,102...) custom-call(bf16[64,16384]{1,0:T(8,128)(2,1)} %refs_0_.1, ...), custom_call_target="tpu_custom_call" | custom-call | tf_op jit(solution)/shard_map/pallas_call | solution.py:663
  106.1 2.4 %shard_map.78 = (f32[512,1024]{1,0:T(8,128)}, f32[512,1024]{1,0:T(8,128)}) custom-call(f32[128,1024]{1,0:T(8,128)S(1)} %get-tuple-element.16.refs_0_, f32[128,1024]{1,0:T(8,128)S(1)} %get-tuple-element.17.refs_1_, f32[128,1024]{1,0:T(8,128)S(1)} %get-tuple-element.18.refs_2_, f32[128,1024]{1,0:T(8,128)S(1)} %get-tuple-element.19.refs_3_, ...), custom_call_target="tpu_custom_call" | custom-call | tf_op jit(solution)/shard_map/pallas_call | solution.py:716
  (1 shorter events, 0.0 us)
